TPU v7x, 32 devices: a whole 2x2x4 slice. The times are simulated.
32 devices in a mesh: node: 16 (over z, x, core), head: 2 (over y).
Axes of the slice: x: 2, y: 2, z: 4, core: 2. Of those that a mesh axis runs over, the one named last changes fastest.
Arguments:
- features: bfloat16 [32768, 100], P('node'), may hold values from -6 to 6
- proj_weight: bfloat16 [100, 512], P(None, 'head'), may hold values from -0.625 to 0.625
- score_src: float32 [8, 64], P('head'), may hold values from -150 to 150
- score_dst: float32 [8, 64], P('head'), may hold values from -0.75 to 0.75
- request_rows: int32 [16, 16, 512], P('node'), may hold values from 0 to 2047
- slot_index: int32 [8192, 16], P('node'), may hold values from 0 to 8191
- slot_count: int32 [8192], P('node'), may hold values from 1 to 16
- out_weight: bfloat16 [512, 512], replicated, may hold values from -0.25 to 0.25
Outputs:
- layer_out: bfloat16 [8192, 512], P(('node', 'head'))
All inputs are finite; a program needn't handle non-finite values.
Results may differ from a plain program's by a relative error of at most 0.012.
The roundings to bfloat16 on the way count: a program that leaves them out, or rounds other values in their place, can miss the bound.
Values may be sent and summed in bfloat16 or wider, within the bound.
No kernel may reach another device: no remote copies, remote signals or barrier semaphores. Data moves between devices by JAX's collectives and lax.ppermute only.
A program may use at most 64 MiB of HBM per device.

v0:
```python
import math

import jax
import jax.numpy as jnp
from jax import lax
from jax.sharding import PartitionSpec as P


def pick_rows(table, row_index):
    total = row_index.shape[0]
    block_rows = math.gcd(total, 1024)
    columns = lax.iota(jnp.int32, table.shape[0])

    def select_block(row_ids):
        hot_table = (row_ids[:, None] == columns[None, :]).astype(table.dtype)
        return jnp.dot(hot_table, table, preferred_element_type=jnp.float32).astype(table.dtype)

    chosen = lax.map(select_block, row_index.reshape(total // block_rows, block_rows))
    return chosen.reshape(total, table.shape[1])


def local(
    features, proj_weight, score_src, score_dst, request_rows, slot_index, slot_count, out_weight
):
    groups = lax.axis_size("node")
    capacity = request_rows.shape[2]
    width = proj_weight.shape[1]
    local_heads = score_src.shape[0]
    head_dim = score_src.shape[1]
    dst_rows = slot_index.shape[0]
    slot_total = slot_index.shape[1]
    wanted = lax.all_to_all(request_rows, "node", split_axis=1, concat_axis=0, tiled=True).reshape(
        groups * capacity
    )
    picked = pick_rows(features, wanted)
    fetched = jnp.einsum(
        "ocf,fw->ocw",
        lax.all_to_all(
            picked.reshape(groups, capacity, features.shape[1]),
            "node",
            split_axis=0,
            concat_axis=0,
            tiled=True,
        ),
        proj_weight,
        preferred_element_type=jnp.float32,
    ).astype(jnp.bfloat16)
    buffer_rows = fetched.reshape(groups * capacity, width)
    zvals = pick_rows(buffer_rows, slot_index.reshape(-1)).reshape(
        dst_rows, slot_total, local_heads, head_dim
    )
    src_part = jnp.einsum("rshd,hd->rsh", zvals.astype(jnp.float32), score_src)
    dst_part = jnp.einsum("rhd,hd->rh", zvals[:, 0].astype(jnp.float32), score_dst)
    logit = src_part + dst_part[:, None, :]
    logit = jnp.where(logit > 0, logit, 0.2 * logit)
    live_mask = (jnp.arange(slot_total, dtype=jnp.int32)[None, :] < slot_count[:, None])[:, :, None]
    logit = jnp.where(live_mask, logit, -1e30)
    peak = jnp.max(logit, axis=1, keepdims=True)
    weights = jnp.where(live_mask, jnp.exp(logit - peak), 0.0)
    alpha = (weights / jnp.sum(weights, axis=1, keepdims=True)).astype(jnp.bfloat16)
    summed = jnp.einsum("rsh,rshd->rhd", alpha, zvals, preferred_element_type=jnp.float32)
    hidden = jax.nn.elu(summed).astype(jnp.bfloat16).reshape(dst_rows, local_heads * head_dim)
    gathered = lax.all_to_all(hidden, "head", split_axis=0, concat_axis=1, tiled=True)
    layer_out = jnp.dot(gathered, out_weight, preferred_element_type=jnp.float32).astype(
        jnp.bfloat16
    )
    return layer_out


def solution(mesh):
    in_specs = (
        P("node", None),
        P(None, "head"),
        P("head", None),
        P("head", None),
        P("node", None, None),
        P("node", None),
        P("node"),
        P(),
    )
    out_specs = P(("node", "head"), None)
    return jax.shard_map(local, mesh=mesh, in_specs=in_specs, out_specs=out_specs, check_vma=False)
```

profile of v0, /device:TPU:10, one launch (start us, length us, event | category | flops | bytes accessed | tf_op | source)
XLA Modules:
  0.0 219.4 jit_solution(17410106399301376929)
XLA Ops:
  1.5 6.2 %all-to-all-start = ((s32[1,16,512]{2,0,1:T(1,128)}), s32[1,16,512]{2,0,1:T(1,128)S(1)}, u32[]{:S(2)}, u32[]{:S(2)}) async-start(s32[1,16,512]{2,0,1:T(1,128)} %copy.25), calls=%async_computation | async-start | bytes 65536 | tf_op jit(solution)/shard_map/all_to_all | solution.py:32
  7.7 4.2 %all-to-all-done = s32[1,16,512]{2,0,1:T(1,128)S(1)} async-done(((s32[1,16,512]{2,0,1:T(1,128)}), s32[1,16,512]{2,0,1:T(1,128)S(1)}, u32[]{:S(2)}, u32[]{:S(2)}) %all-to-all-start) | async-done | bytes 32800 | tf_op jit(solution)/shard_map/all_to_all | solution.py:32
  12.0 28.4 %while.22 = (s32[]{:T(128)}, bf16[8,1024,100]{1,2,0:T(8,128)(2,1)}, s32[8,1024]{1,0:T(8,128)S(1)}, bf16[2048,100]{0,1:T(8,128)(2,1)}, s32[]{:T(128)}) while((s32[]{:T(128)}, bf16[8,1024,100]{1,2,0:T(8,128)(2,1)}, s32[8,1024]{1,0:T(8,128)S(1)}, bf16[2048,100]{0,1:T(8,128)(2,1)}, s32[]{:T(128)}) %tuple.37), condition=%wide.region_1.2_spmd.clone, body=%wide.region_0.1_spmd.clone.sunk | while | flops 421629952 | bytes 651341 | solution.py:18
  15.6 3.5 %fusion.59 = bf16[8,1024,100]{1,2,0:T(8,128)(2,1)} fusion(bf16[8,1024,100]{1,2,0:T(8,128)(2,1)} %get-tuple-element.153, s32[]{:T(128)S(6)} %copy.58, bf16[2048,100]{0,1:T(8,128)(2,1)} %get-tuple-element.160, s32[1024]{0:T(1024)S(1)} %bitcast.68), kind=kOutput, calls=%fused_computation.7.clone.1 | convolution fusion | flops 421629952 | bytes 643076 | tf_op jit(solution)/shard_map/while/body/eval_jaxpr/dot_general | solution.py:16
  19.1 3.5 %fusion.59 = bf16[8,1024,100]{1,2,0:T(8,128)(2,1)} fusion(bf16[8,1024,100]{1,2,0:T(8,128)(2,1)} %get-tuple-element.153, s32[]{:T(128)S(6)} %copy.58, bf16[2048,100]{0,1:T(8,128)(2,1)} %get-tuple-element.160, s32[1024]{0:T(1024)S(1)} %bitcast.68), kind=kOutput, calls=%fused_computation.7.clone.1 | convolution fusion | flops 421629952 | bytes 643076 | tf_op jit(solution)/shard_map/while/body/eval_jaxpr/dot_general | solution.py:16
  26.2 3.5 %fusion.59 = bf16[8,1024,100]{1,2,0:T(8,128)(2,1)} fusion(bf16[8,1024,100]{1,2,0:T(8,128)(2,1)} %get-tuple-element.153, s32[]{:T(128)S(6)} %copy.58, bf16[2048,100]{0,1:T(8,128)(2,1)} %get-tuple-element.160, s32[1024]{0:T(1024)S(1)} %bitcast.68), kind=kOutput, calls=%fused_computation.7.clone.1 | convolution fusion | flops 421629952 | bytes 643076 | tf_op jit(solution)/shard_map/while/body/eval_jaxpr/dot_general | solution.py:16
  29.8 3.5 %fusion.59 = bf16[8,1024,100]{1,2,0:T(8,128)(2,1)} fusion(bf16[8,1024,100]{1,2,0:T(8,128)(2,1)} %get-tuple-element.153, s32[]{:T(128)S(6)} %copy.58, bf16[2048,100]{0,1:T(8,128)(2,1)} %get-tuple-element.160, s32[1024]{0:T(1024)S(1)} %bitcast.68), kind=kOutput, calls=%fused_computation.7.clone.1 | convolution fusion | flops 421629952 | bytes 643076 | tf_op jit(solution)/shard_map/while/body/eval_jaxpr/dot_general | solution.py:16
  33.3 3.6 %fusion.59 = bf16[8,1024,100]{1,2,0:T(8,128)(2,1)} fusion(bf16[8,1024,100]{1,2,0:T(8,128)(2,1)} %get-tuple-element.153, s32[]{:T(128)S(6)} %copy.58, bf16[2048,100]{0,1:T(8,128)(2,1)} %get-tuple-element.160, s32[1024]{0:T(1024)S(1)} %bitcast.68), kind=kOutput, calls=%fused_computation.7.clone.1 | convolution fusion | flops 421629952 | bytes 643076 | tf_op jit(solution)/shard_map/while/body/eval_jaxpr/dot_general | solution.py:16
  44.3 3.5 %copy.27 = bf16[16,512,100]{1,2,0:T(8,128)(2,1)} copy(bf16[16,512,100]{1,0,2:T(8,128)(2,1)} %reshape_reshape.14) | data formatting | bytes 3276800 | tf_op jit(solution)/shard_map/reshape;reshape | solution.py:39
  47.8 6.1 %all-to-all-start.1 = ((bf16[16,512,100]{1,2,0:T(8,128)(2,1)}), bf16[16,512,100]{1,2,0:T(8,128)(2,1)S(1)}, u32[]{:S(2)}, u32[]{:S(2)}) async-start(bf16[16,512,100]{1,2,0:T(8,128)(2,1)} %copy.27), calls=%async_computation.1 | async-start | bytes 3407872 | tf_op jit(solution)/shard_map/all_to_all | solution.py:38
  54.2 38.4 %all-to-all-done.1 = bf16[16,512,100]{1,2,0:T(8,128)(2,1)S(1)} async-done(((bf16[16,512,100]{1,2,0:T(8,128)(2,1)}), bf16[16,512,100]{1,2,0:T(8,128)(2,1)S(1)}, u32[]{:S(2)}, u32[]{:S(2)}) %all-to-all-start.1) | async-done | bytes 1638432 | tf_op jit(solution)/shard_map/all_to_all | solution.py:38
  95.9 67.8 %while.23 = (s32[]{:T(128)}, bf16[8,1024,256]{2,1,0:T(8,128)(2,1)}, s32[8,1024]{1,0:T(8,128)S(1)}, bf16[8192,256]{1,0:T(8,128)(2,1)}, s32[]{:T(128)}) while((s32[]{:T(128)}, bf16[8,1024,256]{2,1,0:T(8,128)(2,1)}, s32[8,1024]{1,0:T(8,128)S(1)}, bf16[8192,256]{1,0:T(8,128)(2,1)}, s32[]{:T(128)}) %tuple.43), condition=%wide.region_3.4_spmd.clone, body=%wide.region_2.3_spmd.clone.sunk | while | flops 4303618048 | bytes 4730957 | solution.py:18
  95.9 8.5 %fusion.61 = bf16[8,1024,256]{2,1,0:T(8,128)(2,1)} fusion(bf16[8,1024,256]{2,1,0:T(8,128)(2,1)} %get-tuple-element.168, s32[]{:T(128)S(6)} %copy.64, bf16[8192,256]{1,0:T(8,128)(2,1)} %get-tuple-element.175, s32[1024]{0:T(1024)S(1)} %bitcast.69), kind=kOutput, calls=%fused_computation.14.clone.1 | convolution fusion | flops 4303618048 | bytes 4722692 | tf_op jit(solution)/shard_map/while/body/eval_jaxpr/dot_general | solution.py:16
  104.5 8.5 %fusion.61 = bf16[8,1024,256]{2,1,0:T(8,128)(2,1)} fusion(bf16[8,1024,256]{2,1,0:T(8,128)(2,1)} %get-tuple-element.168, s32[]{:T(128)S(6)} %copy.64, bf16[8192,256]{1,0:T(8,128)(2,1)} %get-tuple-element.175, s32[1024]{0:T(1024)S(1)} %bitcast.69), kind=kOutput, calls=%fused_computation.14.clone.1 | convolution fusion | flops 4303618048 | bytes 4722692 | tf_op jit(solution)/shard_map/while/body/eval_jaxpr/dot_general | solution.py:16
  113.0 8.4 %fusion.61 = bf16[8,1024,256]{2,1,0:T(8,128)(2,1)} fusion(bf16[8,1024,256]{2,1,0:T(8,128)(2,1)} %get-tuple-element.168, s32[]{:T(128)S(6)} %copy.64, bf16[8192,256]{1,0:T(8,128)(2,1)} %get-tuple-element.175, s32[1024]{0:T(1024)S(1)} %bitcast.69), kind=kOutput, calls=%fused_computation.14.clone.1 | convolution fusion | flops 4303618048 | bytes 4722692 | tf_op jit(solution)/shard_map/while/body/eval_jaxpr/dot_general | solution.py:16
  121.5 8.4 %fusion.61 = bf16[8,1024,256]{2,1,0:T(8,128)(2,1)} fusion(bf16[8,1024,256]{2,1,0:T(8,128)(2,1)} %get-tuple-element.168, s32[]{:T(128)S(6)} %copy.64, bf16[8192,256]{1,0:T(8,128)(2,1)} %get-tuple-element.175, s32[1024]{0:T(1024)S(1)} %bitcast.69), kind=kOutput, calls=%fused_computation.14.clone.1 | convolution fusion | flops 4303618048 | bytes 4722692 | tf_op jit(solution)/shard_map/while/body/eval_jaxpr/dot_general | solution.py:16
  129.9 8.5 %fusion.61 = bf16[8,1024,256]{2,1,0:T(8,128)(2,1)} fusion(bf16[8,1024,256]{2,1,0:T(8,128)(2,1)} %get-tuple-element.168, s32[]{:T(128)S(6)} %copy.64, bf16[8192,256]{1,0:T(8,128)(2,1)} %get-tuple-element.175, s32[1024]{0:T(1024)S(1)} %bitcast.69), kind=kOutput, calls=%fused_computation.14.clone.1 | convolution fusion | flops 4303618048 | bytes 4722692 | tf_op jit(solution)/shard_map/while/body/eval_jaxpr/dot_general | solution.py:16
  138.4 8.5 %fusion.61 = bf16[8,1024,256]{2,1,0:T(8,128)(2,1)} fusion(bf16[8,1024,256]{2,1,0:T(8,128)(2,1)} %get-tuple-element.168, s32[]{:T(128)S(6)} %copy.64, bf16[8192,256]{1,0:T(8,128)(2,1)} %get-tuple-element.175, s32[1024]{0:T(1024)S(1)} %bitcast.69), kind=kOutput, calls=%fused_computation.14.clone.1 | convolution fusion | flops 4303618048 | bytes 4722692 | tf_op jit(solution)/shard_map/while/body/eval_jaxpr/dot_general | solution.py:16
  146.9 8.4 %fusion.61 = bf16[8,1024,256]{2,1,0:T(8,128)(2,1)} fusion(bf16[8,1024,256]{2,1,0:T(8,128)(2,1)} %get-tuple-element.168, s32[]{:T(128)S(6)} %copy.64, bf16[8192,256]{1,0:T(8,128)(2,1)} %get-tuple-element.175, s32[1024]{0:T(1024)S(1)} %bitcast.69), kind=kOutput, calls=%fused_computation.14.clone.1 | convolution fusion | flops 4303618048 | bytes 4722692 | tf_op jit(solution)/shard_map/while/body/eval_jaxpr/dot_general | solution.py:16
  155.3 8.5 %fusion.61 = bf16[8,1024,256]{2,1,0:T(8,128)(2,1)} fusion(bf16[8,1024,256]{2,1,0:T(8,128)(2,1)} %get-tuple-element.168, s32[]{:T(128)S(6)} %copy.64, bf16[8192,256]{1,0:T(8,128)(2,1)} %get-tuple-element.175, s32[1024]{0:T(1024)S(1)} %bitcast.69), kind=kOutput, calls=%fused_computation.14.clone.1 | convolution fusion | flops 4303618048 | bytes 4722692 | tf_op jit(solution)/shard_map/while/body/eval_jaxpr/dot_general | solution.py:16
  163.8 12.9 %reshape_reshape.15 = bf16[512,16,4,64]{3,2,1,0:T(4,128)(2,1)} reshape(bf16[8,1024,256]{2,1,0:T(8,128)(2,1)} %get-tuple-element.60) | data formatting | bytes 8388608 | tf_op jit(solution)/shard_map/reshape;reshape | solution.py:49
  178.2 13.0 %multiply_reduce_fusion.1 = f32[4,512,16]{0,2,1:T(8,128)} fusion(f32[4,64]{1,0:T(4,128)S(1)} %copy-done.4, bf16[512,16,4,64]{3,2,1,0:T(4,128)(2,1)} %reshape_reshape.15), kind=kLoop, calls=%fused_computation.19 | loop fusion | flops 6258688 | bytes 4326400
  197.6 11.7 %multiply_reduce_fusion = f32[512,4,64]{2,1,0:T(4,128)S(1)} fusion(f32[512,4,16]{1,2,0:T(8,128)} %copy.48, bf16[512,16,4,64]{3,2,1,0:T(4,128)(2,1)} %reshape_reshape.15), kind=kLoop, calls=%fused_computation.18 | loop fusion | flops 6160384 | bytes 4849664
  210.0 8.4 %all_to_all.33 = bf16[2,256,256]{1,2,0:T(8,128)(2,1)S(1)} all-to-all(bf16[2,256,256]{1,2,0:T(8,128)(2,1)S(1)} %copy.28), channel_id=1, replica_groups=mesh['node'=16,'head'=2] {'head'}, dimensions={0} | all-to-all | bytes 524288 | tf_op jit(solution)/shard_map/all_to_all | solution.py:63
  (53 shorter events, 29.3 us)
Async XLA Ops:
  0.0 218.4 %copy-start = (bf16[512,512]{1,0:T(8,128)(2,1)S(1)}, bf16[512,512]{1,0:T(8,128)(2,1)}, u32[]{:S(2)}) copy-start(bf16[512,512]{1,0:T(8,128)(2,1)} %param.19) | copy-start | bytes 1572868
  1.5 10.4 %all-to-all-start = ((s32[1,16,512]{2,0,1:T(1,128)}), s32[1,16,512]{2,0,1:T(1,128)S(1)}, u32[]{:S(2)}, u32[]{:S(2)}) async-start(s32[1,16,512]{2,0,1:T(1,128)} %copy.25), calls=%async_computation | async-start | bytes 65536 | tf_op jit(solution)/shard_map/all_to_all | solution.py:32
  44.3 9.6 %copy-start.2 = (s32[512,16]{0,1:T(8,128)S(1)}, s32[512,16]{0,1:T(8,128)}, u32[]{:S(2)}) copy-start(s32[512,16]{0,1:T(8,128)} %param.17) | copy-start | bytes 98308
  44.3 9.9 %copy-start.3 = (s32[512]{0:T(512)S(1)}, s32[512]{0:T(512)}, u32[]{:S(2)}) copy-start(s32[512]{0:T(512)} %param.18) | copy-start | bytes 6148
  44.3 48.4 %copy-start.1 = (bf16[100,256]{1,0:T(8,128)(2,1)S(1)}, bf16[100,256]{1,0:T(8,128)(2,1)}, u32[]{:S(2)}) copy-start(bf16[100,256]{1,0:T(8,128)(2,1)} %param.13) | copy-start | bytes 153604
  47.8 44.8 %all-to-all-start.1 = ((bf16[16,512,100]{1,2,0:T(8,128)(2,1)}), bf16[16,512,100]{1,2,0:T(8,128)(2,1)S(1)}, u32[]{:S(2)}, u32[]{:S(2)}) async-start(bf16[16,512,100]{1,2,0:T(8,128)(2,1)} %copy.27), calls=%async_computation.1 | async-start | bytes 3407872 | tf_op jit(solution)/shard_map/all_to_all | solution.py:38
  163.8 14.1 %copy-start.5 = (f32[4,64]{1,0:T(4,128)S(1)}, f32[4,64]{1,0:T(4,128)}, u32[]{:S(2)}) copy-start(f32[4,64]{1,0:T(4,128)} %param.15) | copy-start | bytes 3076
  163.8 14.4 %copy-start.4 = (f32[4,64]{1,0:T(4,128)S(1)}, f32[4,64]{1,0:T(4,128)}, u32[]{:S(2)}) copy-start(f32[4,64]{1,0:T(4,128)} %param.14) | copy-start | bytes 3076
where the time goes:
time: 221 us; the launch traced here: 219 us
  matrix products  101 us (46%)
  waiting for transfers between devices  42.6 us (19%)
  local copies, waits for them, and re-layouts  30.2 us (14%)
  other arithmetic  25 us (11%)
  starting transfers between devices  12.3 us (6%)
  blocking collectives  8.39 us (4%)
    dot_general x16, matrix products, select_block(): jnp.dot(hot_table, table, preferred_element_type=jnp.float32)  96.1 us
    all_to_all x1, waiting for transfers between devices, local(): lax.all_to_all(picked.reshape(groups, capacity, features.shape[1]), 'node...  38.4 us
    unnamed x2, other arithmetic  24.7 us
    another operation x1, local copies, waits for them, and re-layouts, local(): pick_rows(buffer_rows, slot_index.reshape(-1))  12.9 us
    all_to_all x1, blocking collectives, local(): lax.all_to_all(hidden, 'head', split_axis=0, concat_axis=1, tiled=True)  8.39 us
    all_to_all x1, starting transfers between devices, local(): lax.all_to_all(request_rows, 'node', split_axis=1, concat_axis=0, tiled=T...  6.24 us
    all_to_all x1, starting transfers between devices, local(): lax.all_to_all(picked.reshape(groups, capacity, features.shape[1]), 'node...  6.07 us
    unnamed x15, local copies, waits for them, and re-layouts  5.08 us
  transfers between devices with their start and end apart: 2, of which 2 were waited for; matrix products, arithmetic and copies ran while one was open for 0% of the time, Pallas kernels for 0%

commit v1 on v0

v1 whole, which is shorter than its diff:
```python
import functools

import jax
import jax.numpy as jnp
from jax import lax
from jax.experimental import pallas as pl
from jax.experimental.pallas import tpu as pltpu
from jax.sharding import PartitionSpec as P

LANES = 128
UNROLL = 32


def spare_split(capacity, feat):
    tucked = capacity * 3 // 16
    piece = -(-feat // 4)
    if tucked % 8 or (capacity - tucked) % 16 or feat + piece > LANES:
        return capacity, 0, piece
    return capacity - tucked, tucked, piece


def copy_rows(index, start, table, out, count):
    unroll = min(UNROLL, count)

    @pl.loop(0, count // unroll)
    def _(step):
        base = pl.multiple_of(step * unroll, unroll)
        for offset in range(unroll):
            row = index[start + base + offset]
            out[pl.ds(base + offset, 1), :] = table[pl.ds(row, 1), :]


def pick_kernel(wanted, features, packed, table, rows, *, whole, tucked, piece):
    feat = features.shape[1]
    capacity = whole + tucked
    table[...] = jnp.zeros(table.shape, jnp.float32)
    table[:, :feat] = features[...].astype(jnp.float32)

    @pl.loop(0, packed.shape[0])
    def _(peer):
        copy_rows(wanted, peer * capacity, table, rows, capacity)
        if tucked:
            lane = lax.broadcasted_iota(jnp.int32, (tucked, LANES), 1)
            extra = rows[whole:, :]
            for part in range(4):
                first = part * tucked
                moved = pltpu.roll(extra, feat - part * piece, axis=1)
                spare = (lane >= feat) & (lane < feat + piece)
                rows[first : first + tucked, :] = jnp.where(
                    spare, moved, rows[first : first + tucked, :]
                )
        packed[peer] = rows[:whole, :].astype(packed.dtype)


def pick_rows(wanted, features, groups):
    capacity = wanted.shape[0] // groups
    whole, tucked, piece = spare_split(capacity, features.shape[1])
    return pl.pallas_call(
        functools.partial(pick_kernel, whole=whole, tucked=tucked, piece=piece),
        grid_spec=pltpu.PrefetchScalarGridSpec(
            num_scalar_prefetch=1,
            grid=(),
            in_specs=[pl.BlockSpec(memory_space=pltpu.VMEM)],
            out_specs=pl.BlockSpec(memory_space=pltpu.VMEM),
            scratch_shapes=[
                pltpu.VMEM((features.shape[0], LANES), jnp.float32),
                pltpu.VMEM((capacity, LANES), jnp.float32),
            ],
        ),
        out_shape=jax.ShapeDtypeStruct((groups, whole, LANES), features.dtype),
        name="pick",
    )(wanted, features)


def attend_kernel(
    slots, packed, weight, scores, spread, counts, out_weight, out, table, rows, hidden,
    *, whole, tucked, piece, feat, heads, block, slot_total
):
    capacity = whole + tucked

    @pl.loop(0, packed.shape[0])
    def _(owner):
        base = pl.multiple_of(owner * capacity, 8)
        sent = packed[owner].astype(jnp.float32)
        table[pl.ds(base, whole), :] = sent
        if tucked:
            lane = lax.broadcasted_iota(jnp.int32, (tucked, LANES), 1)
            extra = jnp.zeros((tucked, LANES), jnp.float32)
            for part in range(4):
                moved = pltpu.roll(
                    sent[part * tucked : (part + 1) * tucked],
                    (LANES - feat + part * piece) % LANES,
                    axis=1,
                )
                extra = jnp.where(
                    (lane >= part * piece) & (lane < (part + 1) * piece), moved, extra
                )
            table[pl.ds(base + whole, tucked), :] = extra

    @pl.loop(0, hidden.shape[0] // block)
    def _(step):
        copy_rows(slots, step * block * slot_total, table, rows, block * slot_total)
        zvals = jnp.dot(
            rows[...].astype(jnp.bfloat16), weight[...], preferred_element_type=jnp.float32
        ).astype(jnp.bfloat16)
        parts = jnp.dot(zvals, scores[...], preferred_element_type=jnp.float32)
        src = (
            parts
            + pltpu.roll(parts, LANES - heads, axis=1)
            + pltpu.roll(parts, LANES - 2 * heads, axis=1)
        )
        dst = pltpu.roll(src[:block], LANES - 3 * heads, axis=1)
        live = jnp.broadcast_to(
            counts[pl.ds(pl.multiple_of(step * block, 8), block), :], (block, LANES)
        )
        logits = []
        for slot in range(slot_total):
            logit = src[slot * block : (slot + 1) * block] + dst
            logit = jnp.where(logit > 0, logit, 0.2 * logit)
            logits.append(jnp.where(live > slot, logit, -1e30))
        peak = functools.reduce(jnp.maximum, logits)
        shares = [
            jnp.where(live > slot, jnp.exp(logit - peak), 0.0)
            for slot, logit in enumerate(logits)
        ]
        scale = 1.0 / functools.reduce(jnp.add, shares)
        alpha = jnp.concatenate([share * scale for share in shares], axis=0)
        wide = jnp.dot(
            alpha.astype(jnp.bfloat16), spread[...], preferred_element_type=jnp.float32
        )
        terms = wide * zvals.astype(jnp.float32)
        summed = functools.reduce(
            jnp.add, [terms[slot * block : (slot + 1) * block] for slot in range(slot_total)]
        )
        low = jnp.minimum(summed, 0.0)
        series = low * (1.0 + low * (0.5 + low * (1.0 / 6.0)))
        below = jnp.where(low > -0.01, series, jnp.exp(low) - 1.0)
        hidden[pl.ds(pl.multiple_of(step * block, 8), block), :] = jnp.where(
            summed > 0, summed, below
        )

    out[...] = jnp.dot(
        hidden[...].astype(jnp.bfloat16), out_weight[...], preferred_element_type=jnp.float32
    ).astype(out.dtype)


def attend(packed, slots, weight, scores, spread, counts, out_weight, capacity, feat, heads, block):
    whole, tucked, piece = spare_split(capacity, feat)
    dst_rows = counts.shape[0]
    slot_total = slots.shape[0] // dst_rows
    width = weight.shape[1]
    return pl.pallas_call(
        functools.partial(
            attend_kernel,
            whole=whole,
            tucked=tucked,
            piece=piece,
            feat=feat,
            heads=heads,
            block=block,
            slot_total=slot_total,
        ),
        grid_spec=pltpu.PrefetchScalarGridSpec(
            num_scalar_prefetch=1,
            grid=(),
            in_specs=[pl.BlockSpec(memory_space=pltpu.VMEM)] * 6,
            out_specs=pl.BlockSpec(memory_space=pltpu.VMEM),
            scratch_shapes=[
                pltpu.VMEM((packed.shape[0] * capacity, LANES), jnp.float32),
                pltpu.VMEM((block * slot_total, LANES), jnp.float32),
                pltpu.VMEM((dst_rows, width), jnp.float32),
            ],
        ),
        out_shape=jax.ShapeDtypeStruct((dst_rows, out_weight.shape[1]), jnp.bfloat16),
        name="attend",
    )(slots, packed, weight, scores, spread, counts, out_weight)


def three_pieces(values):
    high = lax.reduce_precision(values, 8, 7)
    rest = values - high
    middle = lax.reduce_precision(rest, 8, 7)
    return [piece.astype(jnp.bfloat16) for piece in (high, middle, rest - middle)]


def local(
    features, proj_weight, score_src, score_dst, request_rows, slot_index, slot_count, out_weight
):
    groups = lax.axis_size("node")
    sides = lax.axis_size("head")
    side = lax.axis_index("head")
    capacity = request_rows.shape[2]
    feat = features.shape[1]
    local_heads, head_dim = score_src.shape
    heads = local_heads * sides
    slot_total = slot_index.shape[1]
    dst_rows = slot_index.shape[0] // sides
    block = min(32, dst_rows)

    wanted = lax.all_to_all(request_rows, "node", split_axis=1, concat_axis=0, tiled=True).reshape(
        groups * capacity
    )

    pieces = [
        piece.reshape(1, -1) for score in (score_src, score_dst) for piece in three_pieces(score)
    ]
    mine = jnp.concatenate([proj_weight] + pieces, axis=0)
    both = lax.all_gather(mine, "head", axis=0, tiled=False)
    both = jnp.transpose(both, (1, 0, 2)).reshape(mine.shape[0], -1)
    weight = jnp.pad(both[:feat], ((0, LANES - feat), (0, 0)))
    column = lax.broadcasted_iota(jnp.int32, (heads * head_dim, LANES), 1)
    owner = lax.broadcasted_iota(jnp.int32, (heads * head_dim, LANES), 0) // head_dim
    scores = jnp.zeros((heads * head_dim, LANES), jnp.bfloat16)
    for rank in range(len(pieces)):
        scores = jnp.where(column == rank * heads + owner, both[feat + rank][:, None], scores)
    spread = (
        lax.broadcasted_iota(jnp.int32, (LANES, heads * head_dim), 0)
        == lax.broadcasted_iota(jnp.int32, (LANES, heads * head_dim), 1) // head_dim
    ).astype(jnp.bfloat16)

    slots = lax.dynamic_slice_in_dim(slot_index, side * dst_rows, dst_rows, 0)
    slots = jnp.transpose(
        slots.reshape(dst_rows // block, block, slot_total), (0, 2, 1)
    ).reshape(-1)
    counts = lax.dynamic_slice_in_dim(slot_count, side * dst_rows, dst_rows, 0)[:, None]

    picked = pick_rows(wanted, features, groups)
    fetched = lax.all_to_all(picked, "node", split_axis=0, concat_axis=0, tiled=True)
    return attend(
        fetched, slots, weight, scores, spread, counts, out_weight, capacity, feat, heads, block
    )


def solution(mesh):
    in_specs = (
        P("node", None),
        P(None, "head"),
        P("head", None),
        P("head", None),
        P("node", None, None),
        P("node", None),
        P("node"),
        P(),
    )
    out_specs = P(("node", "head"), None)
    return jax.shard_map(local, mesh=mesh, in_specs=in_specs, out_specs=out_specs, check_vma=False)
```

time: 221 us -> 90.4 us (0.41)
  matrix products: 101 us -> 0 us
  Pallas kernels: 0 us -> 30.6 us
  other arithmetic: 25 us -> 2.1 us
  local copies, waits for them, and re-layouts: 30.2 us -> 8.4 us
  waiting for transfers between devices: 42.6 us -> 30.7 us
  blocking collectives: 8.39 us -> 4.83 us
    dot_general x19 -> x0, matrix products: 101 us -> none  [the longest x16 96.1 us: select_block(): jnp.dot(hot_table, table, preferred_element_type=jnp.float32)]
    pallas_call x0 -> x2, Pallas kernels: none -> 30.6 us  [the longest x1 17.7 us: attend(): pl.pallas_call(functools.partial(attend_kernel, whole=whole, tucked=tucke...]
    unnamed x2 -> x0, other arithmetic: 24.7 us -> none
    another operation x5 -> x0, local copies, waits for them, and re-layouts: 18.1 us -> none  [the longest x1 12.9 us: local(): pick_rows(buffer_rows, slot_index.reshape(-1))]
    all_to_all x1, waiting for transfers between devices: 38.4 us -> 28.5 us  [local(): lax.all_to_all(picked, 'node', split_axis=0, concat_axis=0, tiled=True)]
    all_to_all x1 -> x0, blocking collectives: 8.39 us -> none  [local(): lax.all_to_all(hidden, 'head', split_axis=0, concat_axis=1, tiled=True)]
    all_gather x0 -> x1, blocking collectives: none -> 4.83 us  [local(): both = lax.all_gather(mine, 'head', axis=0, tiled=False)]
    dot_general x3 -> x0, local copies, waits for them, and re-layouts: 3.22 us -> none  [the longest x1 2.87 us: local(): src_part = jnp.einsum('rshd,hd->rsh', zvals.astype(jnp.float32), score_src)]
  transfers between devices with their start and end apart: 2 -> 2, of which waited for: 2 -> 2; matrix products, arithmetic and copies ran while one was open for 0% -> 8% of each run, Pallas kernels for 0% -> 0%
where the time goes in v1:
time: 90.4 us; the launch traced here: 89.2 us
  waiting for transfers between devices  30.7 us (34%)
  Pallas kernels  30.6 us (34%)
  starting transfers between devices  12.4 us (14%)
  local copies, waits for them, and re-layouts  8.4 us (9%)
  blocking collectives  4.83 us (5%)
  other arithmetic  2.1 us (2%)
    all_to_all x1, waiting for transfers between devices, local(): lax.all_to_all(picked, 'node', split_axis=0, concat_axis=0, tiled=True)  28.5 us
    pallas_call x1, Pallas kernels, attend(): pl.pallas_call(functools.partial(attend_kernel, whole=whole, tucked=tucke...  17.7 us
    pallas_call x1, Pallas kernels, pick_rows(): pl.pallas_call(functools.partial(pick_kernel, whole=whole, tucked=tucked,...  12.9 us
    all_to_all x1, starting transfers between devices, local(): lax.all_to_all(request_rows, 'node', split_axis=1, concat_axis=0, tiled=T...  6.24 us
    all_to_all x1, starting transfers between devices, local(): lax.all_to_all(picked, 'node', split_axis=0, concat_axis=0, tiled=True)  6.2 us
    unnamed x24, local copies, waits for them, and re-layouts  5.4 us
    all_gather x1, blocking collectives, local(): both = lax.all_gather(mine, 'head', axis=0, tiled=False)  4.83 us
    all_to_all x1, waiting for transfers between devices, local(): lax.all_to_all(request_rows, 'node', split_axis=1, concat_axis=0, tiled=T...  2.15 us
  transfers between devices with their start and end apart: 2, of which 2 were waited for; matrix products, arithmetic and copies ran while one was open for 8% of the time, Pallas kernels for 0%

profile of v1, /device:TPU:10, one launch (start us, length us, event | category | flops | bytes accessed | tf_op | source)
XLA Modules:
  0.0 89.2 jit_solution(17221652254880646998)
XLA Ops:
  0.0 1.4 %copy.19 = s32[1,16,512]{2,0,1:T(1,128)} copy(s32[1,16,512]{2,1,0:T(8,128)} %param.12) | data formatting | bytes 65536 | tf_op args[4]
  1.4 6.2 %all-to-all-start = ((s32[1,16,512]{2,0,1:T(1,128)}), s32[1,16,512]{2,0,1:T(1,128)S(1)}, u32[]{:S(2)}, u32[]{:S(2)}) async-start(s32[1,16,512]{2,0,1:T(1,128)} %copy.19), calls=%async_computation | async-start | bytes 65536 | tf_op jit(solution)/shard_map/all_to_all | solution.py:200
  7.7 2.0 %copy.20.features = bf16[2048,100]{1,0:T(8,128)(2,1)} copy(bf16[2048,100]{0,1:T(8,128)(2,1)} %param.8) | data formatting | bytes 819200 | tf_op args[0]
  9.7 2.2 %all-to-all-done = s32[1,16,512]{2,0,1:T(1,128)S(1)} async-done(((s32[1,16,512]{2,0,1:T(1,128)}), s32[1,16,512]{2,0,1:T(1,128)S(1)}, u32[]{:S(2)}, u32[]{:S(2)}) %all-to-all-start) | async-done | bytes 32800 | tf_op jit(solution)/shard_map/all_to_all | solution.py:200
  11.9 0.6 copy-done.2
  12.5 12.9 %pick.1 = bf16[16,416,128]{2,1,0:T(8,128)(2,1)} custom-call(s32[8192]{0:T(1024)} %bitcast.28, bf16[2048,100]{1,0:T(8,128)(2,1)} %copy.20.features), custom_call_target="tpu_custom_call" | custom-call | tf_op jit(solution)/shard_map/pick/pallas_call | solution.py:58
  25.4 6.2 %all-to-all-start.1 = ((bf16[16,416,128]{2,1,0:T(8,128)(2,1)}), bf16[16,416,128]{2,1,0:T(8,128)(2,1)S(1)}, u32[]{:S(2)}, u32[]{:S(2)}) async-start(bf16[16,416,128]{2,1,0:T(8,128)(2,1)} %pick.1), calls=%async_computation.1 | async-start | bytes 3407872 | tf_op jit(solution)/shard_map/all_to_all | solution.py:228
  31.8 0.7 reshape.52.slots
  32.4 0.1 reshape.54
  32.5 0.1 reshape.55
  32.6 0.1 reshape.56
  32.7 0.1 reshape.57
  32.8 0.1 reshape.58
  32.9 0.1 reshape.59
  33.0 4.8 %all-gather.1 = bf16[2,106,256]{2,1,0:T(8,128)(2,1)S(1)} all-gather(bf16[1,106,256]{2,1,0:T(8,128)(2,1)S(1)} %bitcast.27), channel_id=2, replica_groups=mesh['node'=16,'head'=2] {'head'}, dimensions={0}, use_global_device_ids=true | all-gather | bytes 162816 | tf_op jit(solution)/shard_map/all_gather | solution.py:208
  37.9 0.1 copy.21
  37.9 0.1 pad.5
  38.1 0.7 pad.4.weight
  38.9 0.8 copy.22.counts
  39.7 0.7 fusion.10.spread
  40.4 1.4 %fusion.9.scores = bf16[512,128]{1,0:T(8,128)(2,1)} fusion(s32[512]{0:T(512)S(1)} %get-tuple-element.17, s32[512]{0:T(512)S(1)} %get-tuple-element.18, pred[512]{0:T(512)(128)(4,1)S(1)} %fusion.16, bf16[512]{0:T(512)(128)(2,1)S(1)} %bitcast.29, bf16[512]{0:T(512)(128)(2,1)S(1)} %bitcast.30, bf16[512]{0:T(512)(128)(2,1)S(1)} %bitcast.31, ...), kind=kLoop, calls=%fused_computation.16 | loop fusion | flops 1179648 | bytes 141824 | tf_op jit(solution)/shard_map/jit(_where)/select_n | solution.py:215
  41.8 28.5 %all-to-all-done.1.packed = bf16[16,416,128]{2,1,0:T(8,128)(2,1)S(1)} async-done(((bf16[16,416,128]{2,1,0:T(8,128)(2,1)}), bf16[16,416,128]{2,1,0:T(8,128)(2,1)S(1)}, u32[]{:S(2)}, u32[]{:S(2)}) %all-to-all-start.1) | async-done | bytes 1703968 | tf_op jit(solution)/shard_map/all_to_all | solution.py:228
  70.4 1.2 %copy-done.1 = bf16[16,416,128]{2,1,0:T(8,128)(2,1)} copy-done((bf16[16,416,128]{2,1,0:T(8,128)(2,1)}, bf16[16,416,128]{2,1,0:T(8,128)(2,1)S(1)}, u32[]{:S(2)}) %copy-start.1) | copy-done | bytes 1703960
  71.5 17.7 %attend.1 = bf16[256,512]{1,0:T(8,128)(2,1)} custom-call(s32[4096]{0:T(1024)} %reshape.52.slots, bf16[16,416,128]{2,1,0:T(8,128)(2,1)} %copy-done.1, bf16[128,512]{1,0:T(8,128)(2,1)} %pad.4.weight, bf16[512,128]{1,0:T(8,128)(2,1)} %fusion.9.scores, bf16[128,512]{1,0:T(8,128)(2,1)} %fusion.10.spread, s32[256,1]{1,0:T(8,128)} %copy.22.counts, ...), custom_call_target="tpu_custom_call" | custom-call | tf_op jit(solution)/shard_map/attend/pallas_call | solution.py:152
  (30 shorter events, 0.4 us)
Async XLA Ops:
  0.0 31.6 %copy-start = (s32[512,16]{0,1:T(8,128)S(1)}, s32[512,16]{0,1:T(8,128)}, u32[]{:S(2)}) copy-start(s32[512,16]{0,1:T(8,128)} %param.13) | copy-start | bytes 98308
  1.4 10.4 %all-to-all-start = ((s32[1,16,512]{2,0,1:T(1,128)}), s32[1,16,512]{2,0,1:T(1,128)S(1)}, u32[]{:S(2)}, u32[]{:S(2)}) async-start(s32[1,16,512]{2,0,1:T(1,128)} %copy.19), calls=%async_computation | async-start | bytes 65536 | tf_op jit(solution)/shard_map/all_to_all | solution.py:200
  11.8 0.6 copy-start.2
  25.4 7.0 %copy-start.4 = (f32[4,64]{1,0:T(4,128)S(1)}, f32[4,64]{1,0:T(4,128)}, u32[]{:S(2)}) copy-start(f32[4,64]{1,0:T(4,128)} %param.10) | copy-start | bytes 3076
  25.4 7.3 %copy-start.5 = (f32[4,64]{1,0:T(4,128)S(1)}, f32[4,64]{1,0:T(4,128)}, u32[]{:S(2)}) copy-start(f32[4,64]{1,0:T(4,128)} %param.11) | copy-start | bytes 3076
  25.4 7.5 %copy-start.3 = (bf16[100,256]{1,0:T(8,128)(2,1)S(1)}, bf16[100,256]{1,0:T(8,128)(2,1)}, u32[]{:S(2)}) copy-start(bf16[100,256]{1,0:T(8,128)(2,1)} %param.9) | copy-start | bytes 153604
  25.4 44.9 %all-to-all-start.1 = ((bf16[16,416,128]{2,1,0:T(8,128)(2,1)}), bf16[16,416,128]{2,1,0:T(8,128)(2,1)S(1)}, u32[]{:S(2)}, u32[]{:S(2)}) async-start(bf16[16,416,128]{2,1,0:T(8,128)(2,1)} %pick.1), calls=%async_computation.1 | async-start | bytes 3407872 | tf_op jit(solution)/shard_map/all_to_all | solution.py:228
  31.6 7.2 %copy-start.6 = (s32[512]{0:T(512)S(1)}, s32[512]{0:T(512)}, u32[]{:S(2)}) copy-start(s32[512]{0:T(512)} %param.14) | copy-start | bytes 6148
  70.4 1.2 %copy-start.1 = (bf16[16,416,128]{2,1,0:T(8,128)(2,1)}, bf16[16,416,128]{2,1,0:T(8,128)(2,1)S(1)}, u32[]{:S(2)}) copy-start(bf16[16,416,128]{2,1,0:T(8,128)(2,1)S(1)} %all-to-all-done.1.packed) | copy-start | bytes 5111812

commit v2 on v1

v2 whole, which is shorter than its diff:
```python
import functools

import jax
import jax.numpy as jnp
from jax import lax
from jax.experimental import pallas as pl
from jax.experimental.pallas import tpu as pltpu
from jax.sharding import PartitionSpec as P

LANES = 128


def spare_split(capacity, feat):
    tucked = capacity * 3 // 16
    piece = -(-feat // 4)
    if tucked % 8 or (capacity - tucked) % 16 or feat + piece > LANES:
        return capacity, 0, piece
    return capacity - tucked, tucked, piece


def copy_rows(index, table, out, count):
    for place in range(count):
        out[place : place + 1, :] = table[pl.ds(index[place], 1), :]


def list_copy(lists, number, buffer, sem, count):
    return pltpu.make_async_copy(lists.at[pl.ds(number * count, count)], buffer, sem)


def in_turn(lists, total, count, even, odd, sems, work):
    list_copy(lists, 0, even, sems.at[0], count).start()

    @pl.loop(0, total // 2)
    def _(pair):
        list_copy(lists, 2 * pair, even, sems.at[0], count).wait()
        list_copy(lists, 2 * pair + 1, odd, sems.at[1], count).start()
        work(2 * pair, even)
        list_copy(lists, 2 * pair + 1, odd, sems.at[1], count).wait()

        @pl.when(pair + 1 < total // 2)
        def _():
            list_copy(lists, 2 * pair + 2, even, sems.at[0], count).start()

        work(2 * pair + 1, odd)


def pick_kernel(wanted, features, packed, table, rows, even, odd, sems, *, whole, tucked, piece):
    feat, nodes = features.shape
    capacity = whole + tucked
    table[...] = jnp.zeros(table.shape, jnp.float32)
    for first in range(0, nodes, LANES):
        last = min(first + LANES, nodes)
        table[first:last, :feat] = features[:, first:last].astype(jnp.float32).T

    def work(peer, buffer):
        copy_rows(buffer, table, rows, capacity)
        if tucked:
            lane = lax.broadcasted_iota(jnp.int32, (tucked, LANES), 1)
            spare = (lane >= feat) & (lane < feat + piece)
            extra = rows[whole:, :]
            for part in range(4):
                first = part * tucked
                moved = pltpu.roll(extra, feat - part * piece, axis=1)
                rows[first : first + tucked, :] = jnp.where(
                    spare, moved, rows[first : first + tucked, :]
                )
        packed[peer] = rows[:whole, :].astype(packed.dtype)

    in_turn(wanted, packed.shape[0], capacity, even, odd, sems, work)


def pick_rows(wanted, features, peers):
    capacity = wanted.shape[0] // peers
    feat, nodes = features.shape
    whole, tucked, piece = spare_split(capacity, feat)
    return pl.pallas_call(
        functools.partial(pick_kernel, whole=whole, tucked=tucked, piece=piece),
        in_specs=[
            pl.BlockSpec(memory_space=pl.ANY),
            pl.BlockSpec(memory_space=pltpu.VMEM),
        ],
        out_specs=pl.BlockSpec(memory_space=pltpu.VMEM),
        scratch_shapes=[
            pltpu.VMEM((nodes, LANES), jnp.float32),
            pltpu.VMEM((capacity, LANES), jnp.float32),
            pltpu.SMEM((capacity,), jnp.int32),
            pltpu.SMEM((capacity,), jnp.int32),
            pltpu.SemaphoreType.DMA((2,)),
        ],
        out_shape=jax.ShapeDtypeStruct((peers, whole, LANES), features.dtype),
        name="pick",
    )(wanted, features)


def unpack(packed, table, start, *, whole, tucked, piece, feat):
    capacity = whole + tucked

    @pl.loop(0, packed.shape[0])
    def _(owner):
        base = pl.multiple_of(start + owner * capacity, 8)
        sent = packed[owner].astype(jnp.float32)
        table[pl.ds(base, whole), :] = sent
        if tucked:
            lane = lax.broadcasted_iota(jnp.int32, (tucked, LANES), 1)
            extra = jnp.zeros((tucked, LANES), jnp.float32)
            for part in range(4):
                moved = pltpu.roll(
                    sent[part * tucked : (part + 1) * tucked],
                    (LANES - feat + part * piece) % LANES,
                    axis=1,
                )
                extra = jnp.where(
                    (lane >= part * piece) & (lane < (part + 1) * piece), moved, extra
                )
            table[pl.ds(base + whole, tucked), :] = extra


def block_hidden(rows, live, weight, scores, spread, heads, block, slot_total):
    zvals = jnp.dot(
        rows.astype(jnp.bfloat16), weight, preferred_element_type=jnp.float32
    ).astype(jnp.bfloat16)
    parts = jnp.dot(zvals, scores, preferred_element_type=jnp.float32)
    src = (
        parts
        + pltpu.roll(parts, LANES - heads, axis=1)
        + pltpu.roll(parts, LANES - 2 * heads, axis=1)
    )
    dst = pltpu.roll(src[:block], LANES - 3 * heads, axis=1)
    logits = []
    for slot in range(slot_total):
        logit = src[slot * block : (slot + 1) * block] + dst
        logit = jnp.where(logit > 0, logit, 0.2 * logit)
        logits.append(jnp.where(live > slot, logit, -1e30))
    peak = functools.reduce(jnp.maximum, logits)
    shares = [
        jnp.where(live > slot, jnp.exp(logit - peak), 0.0) for slot, logit in enumerate(logits)
    ]
    scale = 1.0 / functools.reduce(jnp.add, shares)
    alpha = jnp.concatenate([share * scale for share in shares], axis=0)
    wide = jnp.dot(alpha.astype(jnp.bfloat16), spread, preferred_element_type=jnp.float32)
    terms = wide * zvals.astype(jnp.float32)
    summed = functools.reduce(
        jnp.add, [terms[slot * block : (slot + 1) * block] for slot in range(slot_total)]
    )
    low = jnp.minimum(summed, 0.0)
    series = low * (1.0 + low * (0.5 + low * (1.0 / 6.0)))
    below = jnp.where(low > -0.01, series, jnp.exp(low) - 1.0)
    return jnp.where(summed > 0, summed, below)


def attend_kernel(
    slots, near, far, weight, scores, spread, counts, out_weight, out,
    table, rows_even, rows_odd, hidden, even, odd, sems,
    *, whole, tucked, piece, feat, heads, block, slot_total
):
    blocks = hidden.shape[0] // block
    count = block * slot_total

    def fetch(number, buffer, sem):
        return pltpu.make_async_copy(slots.at[pl.ds(number * count, count)], buffer, sem)

    fetch(0, even, sems.at[0]).start()
    fetch(1, odd, sems.at[1]).start()
    sizes = dict(whole=whole, tucked=tucked, piece=piece, feat=feat)
    unpack(near, table, 0, **sizes)
    unpack(far, table, near.shape[0] * (whole + tucked), **sizes)

    def compute(number, rows):
        first = pl.multiple_of(number * block, 8)
        live = jnp.broadcast_to(counts[pl.ds(first, block), :], (block, LANES))
        hidden[pl.ds(first, block), :] = block_hidden(
            rows[...], live, weight[...], scores[...], spread[...], heads, block, slot_total
        )

    fetch(0, even, sems.at[0]).wait()
    copy_rows(even, table, rows_even, count)

    @pl.loop(0, blocks // 2)
    def _(pair):
        following = jnp.minimum(2 * pair + 2, blocks - 2)
        fetch(following, even, sems.at[0]).start()
        fetch(2 * pair + 1, odd, sems.at[1]).wait()
        copy_rows(odd, table, rows_odd, count)
        compute(2 * pair, rows_even)
        fetch(following + 1, odd, sems.at[1]).start()
        fetch(following, even, sems.at[0]).wait()
        copy_rows(even, table, rows_even, count)
        compute(2 * pair + 1, rows_odd)

    fetch(blocks - 1, odd, sems.at[1]).wait()
    out[...] = jnp.dot(
        hidden[...].astype(jnp.bfloat16), out_weight[...], preferred_element_type=jnp.float32
    ).astype(out.dtype)


def attend(slots, near, far, weight, scores, spread, counts, out_weight, capacity, feat, heads, block):
    whole, tucked, piece = spare_split(capacity, feat)
    dst_rows = counts.shape[0]
    slot_total = slots.shape[0] // dst_rows
    width = weight.shape[1]
    count = block * slot_total
    return pl.pallas_call(
        functools.partial(
            attend_kernel,
            whole=whole,
            tucked=tucked,
            piece=piece,
            feat=feat,
            heads=heads,
            block=block,
            slot_total=slot_total,
        ),
        in_specs=[pl.BlockSpec(memory_space=pl.ANY)]
        + [pl.BlockSpec(memory_space=pltpu.VMEM)] * 7,
        out_specs=pl.BlockSpec(memory_space=pltpu.VMEM),
        scratch_shapes=[
            pltpu.VMEM((2 * near.shape[0] * capacity, LANES), jnp.float32),
            pltpu.VMEM((count, LANES), jnp.float32),
            pltpu.VMEM((count, LANES), jnp.float32),
            pltpu.VMEM((dst_rows, width), jnp.float32),
            pltpu.SMEM((count,), jnp.int32),
            pltpu.SMEM((count,), jnp.int32),
            pltpu.SemaphoreType.DMA((2,)),
        ],
        out_shape=jax.ShapeDtypeStruct((dst_rows, out_weight.shape[1]), jnp.bfloat16),
        name="attend",
    )(slots, near, far, weight, scores, spread, counts, out_weight)


def three_pieces(values):
    high = lax.reduce_precision(values, 8, 7)
    rest = values - high
    middle = lax.reduce_precision(rest, 8, 7)
    return [piece.astype(jnp.bfloat16) for piece in (high, middle, rest - middle)]


def shared_weights(proj_weight, score_src, score_dst):
    feat = proj_weight.shape[0]
    local_heads, head_dim = score_src.shape
    heads = local_heads * lax.axis_size("head")
    pieces = [
        piece.reshape(1, -1) for score in (score_src, score_dst) for piece in three_pieces(score)
    ]
    mine = jnp.concatenate([proj_weight] + pieces, axis=0)
    both = lax.all_gather(mine, "head", axis=0, tiled=False)
    both = jnp.transpose(both, (1, 0, 2)).reshape(mine.shape[0], -1)
    weight = jnp.pad(both[:feat], ((0, LANES - feat), (0, 0)))
    column = lax.broadcasted_iota(jnp.int32, (heads * head_dim, LANES), 1)
    owner = lax.broadcasted_iota(jnp.int32, (heads * head_dim, LANES), 0) // head_dim
    scores = jnp.zeros((heads * head_dim, LANES), jnp.bfloat16)
    for rank in range(len(pieces)):
        scores = jnp.where(column == rank * heads + owner, both[feat + rank][:, None], scores)
    spread = (
        lax.broadcasted_iota(jnp.int32, (LANES, heads * head_dim), 0)
        == lax.broadcasted_iota(jnp.int32, (LANES, heads * head_dim), 1) // head_dim
    ).astype(jnp.bfloat16)
    return weight, scores, spread, heads


def local(
    features, proj_weight, score_src, score_dst, request_rows, slot_index, slot_count, out_weight
):
    groups = lax.axis_size("node")
    half = groups // 2
    upper = lax.axis_index("node") // half
    halves = [list(range(half)), list(range(half, groups))]
    sides = lax.axis_size("head")
    side = lax.axis_index("head")
    capacity = request_rows.shape[2]
    feat = features.shape[1]
    slot_total = slot_index.shape[1]
    dst_rows = slot_index.shape[0] // sides
    block = min(32, dst_rows // 2)

    own = features.T
    across = lax.ppermute(own, "node", [(i, (i + half) % groups) for i in range(groups)])

    def within(values):
        return lax.all_to_all(
            values, "node", split_axis=0, concat_axis=0, axis_index_groups=halves, tiled=True
        )

    requests = request_rows.reshape(2, half, capacity)
    requests = jnp.where(upper == 0, requests, requests[::-1])
    wanted = within(jnp.transpose(requests, (1, 0, 2)).reshape(half, 2 * capacity // LANES, LANES))
    wanted = wanted.reshape(half, 2, capacity)

    near = within(pick_rows(wanted[:, 0].reshape(-1), own, half))
    far = within(pick_rows(wanted[:, 1].reshape(-1), across, half))

    weight, scores, spread, heads = shared_weights(proj_weight, score_src, score_dst)
    total = groups * capacity
    slots = lax.dynamic_slice_in_dim(slot_index, side * dst_rows, dst_rows, 0)
    slots = slots + upper * (total // 2)
    slots = jnp.where(slots >= total, slots - total, slots)
    slots = jnp.transpose(
        slots.reshape(dst_rows // block, block, slot_total), (0, 2, 1)
    ).reshape(-1)
    counts = lax.dynamic_slice_in_dim(slot_count, side * dst_rows, dst_rows, 0)[:, None]
    return attend(
        slots, near, far, weight, scores, spread, counts, out_weight, capacity, feat, heads, block
    )


def solution(mesh):
    in_specs = (
        P("node", None),
        P(None, "head"),
        P("head", None),
        P("head", None),
        P("node", None, None),
        P("node", None),
        P("node"),
        P(),
    )
    out_specs = P(("node", "head"), None)
    return jax.shard_map(local, mesh=mesh, in_specs=in_specs, out_specs=out_specs, check_vma=False)
```

time: 90.4 us -> 92.6 us (1.024)
  the two profiles are of different devices: /device:TPU:10 before, /device:TPU:0 now
where the time goes in v2:
time: 92.6 us; the launch traced here: 91.6 us
  Pallas kernels  35.2 us (38%)
  waiting for transfers between devices  18.1 us (20%)
  blocking collectives  14.8 us (16%)
  starting transfers between devices  13.2 us (14%)
  local copies, waits for them, and re-layouts  8.04 us (9%)
  other arithmetic  2.15 us (2%)
    pallas_call x2, Pallas kernels, pick_rows(): pl.pallas_call(functools.partial(pick_kernel, whole=whole, tucked=tucked,...  20.9 us
    ppermute x1, waiting for transfers between devices, local(): lax.ppermute(own, 'node', [(i, (i + half) % groups) for i in range(groups)])  16.7 us
    pallas_call x1, Pallas kernels, attend(): pl.pallas_call(functools.partial(attend_kernel, whole=whole, tucked=tucke...  14.3 us
    all_to_all x2, starting transfers between devices, within(): lax.all_to_all(values, 'node', split_axis=0, concat_axis=0, axis_index_gr...  10.5 us
    all_to_all x1, blocking collectives, within(): lax.all_to_all(values, 'node', split_axis=0, concat_axis=0, axis_index_gr...  9.81 us
    all_gather x1, blocking collectives, shared_weights(): both = lax.all_gather(mine, 'head', axis=0, tiled=False)  4.97 us
    unnamed x28, local copies, waits for them, and re-layouts  4.11 us
    ppermute x1, starting transfers between devices, local(): lax.ppermute(own, 'node', [(i, (i + half) % groups) for i in range(groups)])  2.65 us
  transfers between devices with their start and end apart: 3, of which 2 were waited for; matrix products, arithmetic and copies ran while one was open for 6% of the time, Pallas kernels for 11%

profile of v2, /device:TPU:0, one launch (start us, length us, event | category | flops | bytes accessed | tf_op | source)
XLA Modules:
  0.0 91.6 jit_solution(12657395657048372199)
XLA Ops:
  0.0 0.8 copy-done.4
  0.8 0.2 rev.3
  1.1 9.8 %all_to_all.15 = s32[8,8,128]{2,1,0:T(8,128)S(1)} all-to-all(s32[8,8,128]{2,1,0:T(8,128)S(1)} %reshape.56), channel_id=1, replica_groups={{0,2,4,6,8,10,12,14},{16,18,20,22,24,26,28,30},{1,3,5,7,9,11,13,15},{17..., dimensions={0} | all-to-all | bytes 65536 | tf_op jit(solution)/shard_map/all_to_all | solution.py:279
  10.9 0.6 fusion.17
  11.6 10.4 %pick.2 = bf16[8,416,128]{2,1,0:T(8,128)(2,1)} custom-call(s32[4096]{0:T(1024)} %bitcast.40, bf16[100,2048]{1,0:T(8,128)(2,1)} %bitcast.31), custom_call_target="tpu_custom_call" | custom-call | tf_op jit(solution)/shard_map/pick/pallas_call | solution.py:76
  22.0 3.7 %all-to-all-start.1 = ((bf16[8,416,128]{2,1,0:T(8,128)(2,1)}), bf16[8,416,128]{2,1,0:T(8,128)(2,1)S(1)}, u32[]{:S(2)}, u32[]{:S(2)}) async-start(bf16[8,416,128]{2,1,0:T(8,128)(2,1)} %pick.2), calls=%async_computation.1 | async-start | bytes 1703936 | tf_op jit(solution)/shard_map/all_to_all | solution.py:279
  25.7 2.6 %collective-permute-start = (bf16[100,2048]{1,0:T(8,128)(2,1)S(1)}, bf16[100,2048]{1,0:T(8,128)(2,1)S(1)}, u32[]{:S(2)}, u32[]{:S(2)}) collective-permute-start(bf16[100,2048]{1,0:T(8,128)(2,1)S(1)} %bitcast.32), channel_id=1, source_target_pairs={{0,16},{2,18},{4,20},{6,22},{8,24},{10,26},{12,28},{14,30},{16,0},... | collective-permute-start | bytes 1228808 | tf_op jit(solution)/shard_map/ppermute | solution.py:276
  28.4 16.7 %collective-permute-done.features = bf16[100,2048]{1,0:T(8,128)(2,1)S(1)} collective-permute-done((bf16[100,2048]{1,0:T(8,128)(2,1)S(1)}, bf16[100,2048]{1,0:T(8,128)(2,1)S(1)}, u32[]{:S(2)}, u32[]{:S(2)}) %collective-permute-start) | collective-permute-done | bytes 409632 | tf_op jit(solution)/shard_map/ppermute | solution.py:276
  45.1 0.7 copy-done.3
  45.8 10.4 %pick.3 = bf16[8,416,128]{2,1,0:T(8,128)(2,1)} custom-call(s32[4096]{0:T(1024)} %bitcast.39, bf16[100,2048]{1,0:T(8,128)(2,1)} %copy-done.3), custom_call_target="tpu_custom_call" | custom-call | tf_op jit(solution)/shard_map/pick/pallas_call | solution.py:76
  56.3 0.9 %copy-done = bf16[8,416,128]{2,1,0:T(8,128)(2,1)} copy-done((bf16[8,416,128]{2,1,0:T(8,128)(2,1)}, bf16[8,416,128]{2,1,0:T(8,128)(2,1)S(1)}, u32[]{:S(2)}) %copy-start) | copy-done | bytes 851992
  57.2 6.8 %all-to-all-start.2 = ((bf16[8,416,128]{2,1,0:T(8,128)(2,1)}), bf16[8,416,128]{2,1,0:T(8,128)(2,1)S(1)}, u32[]{:S(2)}, u32[]{:S(2)}) async-start(bf16[8,416,128]{2,1,0:T(8,128)(2,1)} %pick.3), calls=%async_computation.2 | async-start | bytes 1703936 | tf_op jit(solution)/shard_map/all_to_all | solution.py:279
  64.2 0.7 reshape.54.slots
  65.0 0.1 reshape.59
  65.1 0.6 copy-done.8
  66.0 5.0 %all-gather.1 = bf16[2,106,256]{2,1,0:T(8,128)(2,1)S(1)} all-gather(bf16[1,106,256]{2,1,0:T(8,128)(2,1)S(1)} %bitcast.36), channel_id=2, replica_groups=mesh['node'=16,'head'=2] {'head'}, dimensions={0}, use_global_device_ids=true | all-gather | bytes 162816 | tf_op jit(solution)/shard_map/all_gather | solution.py:245
  71.2 0.1 pad.5
  71.4 0.7 pad.4.weight
  72.1 0.8 copy.19.counts
  72.9 0.7 fusion.10.spread
  73.6 1.4 %fusion.9.scores = bf16[512,128]{1,0:T(8,128)(2,1)} fusion(s32[512]{0:T(512)S(1)} %get-tuple-element.19, s32[512]{0:T(512)S(1)} %get-tuple-element.20, pred[512]{0:T(512)(128)(4,1)S(1)} %fusion.16, bf16[512]{0:T(512)(128)(2,1)S(1)} %bitcast.46, bf16[512]{0:T(512)(128)(2,1)S(1)} %bitcast.45, bf16[512]{0:T(512)(128)(2,1)S(1)} %bitcast.44, ...), kind=kLoop, calls=%fused_computation.16 | loop fusion | flops 1179648 | bytes 141824 | tf_op jit(solution)/shard_map/jit(_where)/select_n | solution.py:252
  75.0 1.4 %all-to-all-done.2.far = bf16[8,416,128]{2,1,0:T(8,128)(2,1)S(1)} async-done(((bf16[8,416,128]{2,1,0:T(8,128)(2,1)}), bf16[8,416,128]{2,1,0:T(8,128)(2,1)S(1)}, u32[]{:S(2)}, u32[]{:S(2)}) %all-to-all-start.2) | async-done | bytes 852000 | tf_op jit(solution)/shard_map/all_to_all | solution.py:279
  76.4 0.9 copy-done.1
  77.3 14.3 %attend.1 = bf16[256,512]{1,0:T(8,128)(2,1)} custom-call(s32[4096]{0:T(1024)} %reshape.54.slots, bf16[8,416,128]{2,1,0:T(8,128)(2,1)} %copy-done, bf16[8,416,128]{2,1,0:T(8,128)(2,1)} %copy-done.1, bf16[128,512]{1,0:T(8,128)(2,1)} %pad.4.weight, bf16[512,128]{1,0:T(8,128)(2,1)} %fusion.9.scores, bf16[128,512]{1,0:T(8,128)(2,1)} %fusion.10.spread, ...), custom_call_target="tpu_custom_call" | custom-call | tf_op jit(solution)/shard_map/attend/pallas_call | solution.py:202
  (44 shorter events, 1.0 us)
Async XLA Ops:
  0.0 0.8 copy-start.4
  22.0 3.7 %copy-start.2 = (bf16[2048,100]{0,1:T(8,128)(2,1)S(1)}, bf16[2048,100]{0,1:T(8,128)(2,1)}, u32[]{:S(2)}) copy-start(bf16[2048,100]{0,1:T(8,128)(2,1)} %param.8) | copy-start | bytes 1228804
  22.0 34.2 %all-to-all-start.1 = ((bf16[8,416,128]{2,1,0:T(8,128)(2,1)}), bf16[8,416,128]{2,1,0:T(8,128)(2,1)S(1)}, u32[]{:S(2)}, u32[]{:S(2)}) async-start(bf16[8,416,128]{2,1,0:T(8,128)(2,1)} %pick.2), calls=%async_computation.1 | async-start | bytes 1703936 | tf_op jit(solution)/shard_map/all_to_all | solution.py:279
  25.7 19.3 %collective-permute-start = (bf16[100,2048]{1,0:T(8,128)(2,1)S(1)}, bf16[100,2048]{1,0:T(8,128)(2,1)S(1)}, u32[]{:S(2)}, u32[]{:S(2)}) collective-permute-start(bf16[100,2048]{1,0:T(8,128)(2,1)S(1)} %bitcast.32), channel_id=1, source_target_pairs={{0,16},{2,18},{4,20},{6,22},{8,24},{10,26},{12,28},{14,30},{16,0},... | collective-permute-start | bytes 1228808 | tf_op jit(solution)/shard_map/ppermute | solution.py:276
  45.1 0.7 copy-start.3
  56.2 7.8 %copy-start.6 = (s32[512,16]{0,1:T(8,128)S(1)}, s32[512,16]{0,1:T(8,128)}, u32[]{:S(2)}) copy-start(s32[512,16]{0,1:T(8,128)} %param.13) | copy-start | bytes 98308
  56.3 0.9 %copy-start = (bf16[8,416,128]{2,1,0:T(8,128)(2,1)}, bf16[8,416,128]{2,1,0:T(8,128)(2,1)S(1)}, u32[]{:S(2)}) copy-start(bf16[8,416,128]{2,1,0:T(8,128)(2,1)S(1)} %all-to-all-done.1.near) | copy-start | bytes 2555908
  57.2 19.2 %all-to-all-start.2 = ((bf16[8,416,128]{2,1,0:T(8,128)(2,1)}), bf16[8,416,128]{2,1,0:T(8,128)(2,1)S(1)}, u32[]{:S(2)}, u32[]{:S(2)}) async-start(bf16[8,416,128]{2,1,0:T(8,128)(2,1)} %pick.3), calls=%async_computation.2 | async-start | bytes 1703936 | tf_op jit(solution)/shard_map/all_to_all | solution.py:279
  64.2 0.7 copy-start.7
  64.2 1.8 %copy-start.5 = (bf16[100,256]{1,0:T(8,128)(2,1)S(1)}, bf16[100,256]{1,0:T(8,128)(2,1)}, u32[]{:S(2)}) copy-start(bf16[100,256]{1,0:T(8,128)(2,1)} %param.9) | copy-start | bytes 153604
  65.0 0.7 copy-start.8
  71.3 0.7 copy-start.9
  76.4 0.9 copy-start.1

commit v3 on v2

--- a/solution.py
+++ b/solution.py
@@ -1,4 +1,5 @@
 import functools
+import math
 
 import jax
 import jax.numpy as jnp
@@ -7,7 +8,9 @@
 from jax.experimental.pallas import tpu as pltpu
 from jax.sharding import PartitionSpec as P
 
+
 LANES = 128
+DEPTH = 4
 
 
 def spare_split(capacity, feat):
@@ -23,28 +26,29 @@
         out[place : place + 1, :] = table[pl.ds(index[place], 1), :]
 
 
-def list_copy(lists, number, buffer, sem, count):
-    return pltpu.make_async_copy(lists.at[pl.ds(number * count, count)], buffer, sem)
-
-
-def in_turn(lists, total, count, even, odd, sems, work):
-    list_copy(lists, 0, even, sems.at[0], count).start()
-
-    @pl.loop(0, total // 2)
-    def _(pair):
-        list_copy(lists, 2 * pair, even, sems.at[0], count).wait()
-        list_copy(lists, 2 * pair + 1, odd, sems.at[1], count).start()
-        work(2 * pair, even)
-        list_copy(lists, 2 * pair + 1, odd, sems.at[1], count).wait()
-
-        @pl.when(pair + 1 < total // 2)
-        def _():
-            list_copy(lists, 2 * pair + 2, even, sems.at[0], count).start()
-
-        work(2 * pair + 1, odd)
-
-
-def pick_kernel(wanted, features, packed, table, rows, even, odd, sems, *, whole, tucked, piece):
+def in_turn(lists, total, count, buffers, sems, work):
+    depth = len(buffers)
+
+    def fetch(number, turn):
+        source = lists.at[pl.ds(number * count, count)]
+        return pltpu.make_async_copy(source, buffers[turn], sems.at[turn])
+
+    for turn in range(depth):
+        fetch(turn, turn).start()
+
+    @pl.loop(0, total // depth)
+    def _(group):
+        for turn in range(depth):
+            number = group * depth + turn
+            fetch(number, turn).wait()
+            work(number, buffers[turn])
+
+            @pl.when(number + depth < total)
+            def _():
+                fetch(number + depth, turn).start()
+
+
+def pick_kernel(wanted, features, packed, table, rows, *lists, whole, tucked, piece):
     feat, nodes = features.shape
     capacity = whole + tucked
     table[...] = jnp.zeros(table.shape, jnp.float32)
@@ -66,13 +70,14 @@
                 )
         packed[peer] = rows[:whole, :].astype(packed.dtype)
 
-    in_turn(wanted, packed.shape[0], capacity, even, odd, sems, work)
+    in_turn(wanted, packed.shape[0], capacity, lists[:-1], lists[-1], work)
 
 
 def pick_rows(wanted, features, peers):
     capacity = wanted.shape[0] // peers
     feat, nodes = features.shape
     whole, tucked, piece = spare_split(capacity, feat)
+    depth = math.gcd(DEPTH, peers)
     return pl.pallas_call(
         functools.partial(pick_kernel, whole=whole, tucked=tucked, piece=piece),
         in_specs=[
@@ -83,10 +88,9 @@
         scratch_shapes=[
             pltpu.VMEM((nodes, LANES), jnp.float32),
             pltpu.VMEM((capacity, LANES), jnp.float32),
-            pltpu.SMEM((capacity,), jnp.int32),
-            pltpu.SMEM((capacity,), jnp.int32),
-            pltpu.SemaphoreType.DMA((2,)),
-        ],
+        ]
+        + [pltpu.SMEM((capacity,), jnp.int32)] * depth
+        + [pltpu.SemaphoreType.DMA((depth,))],
         out_shape=jax.ShapeDtypeStruct((peers, whole, LANES), features.dtype),
         name="pick",
     )(wanted, features)
@@ -282,10 +286,12 @@
 
     requests = request_rows.reshape(2, half, capacity)
     requests = jnp.where(upper == 0, requests, requests[::-1])
-    wanted = within(jnp.transpose(requests, (1, 0, 2)).reshape(half, 2 * capacity // LANES, LANES))
+    requests = jnp.transpose(requests, (1, 0, 2)).reshape(half, 2 * capacity // LANES, LANES)
+    wanted = within(requests)
     wanted = wanted.reshape(half, 2, capacity)
 
-    near = within(pick_rows(wanted[:, 0].reshape(-1), own, half))
+    picked = pick_rows(wanted[:, 0].reshape(-1), own, half)
+    near = within(picked)
     far = within(pick_rows(wanted[:, 1].reshape(-1), across, half))
 
     weight, scores, spread, heads = shared_weights(proj_weight, score_src, score_dst)

time: 92.6 us -> 83.1 us (0.90)
  Pallas kernels: 35.2 us -> 26 us
    pallas_call x2, Pallas kernels: 20.9 us -> 11.7 us  [pick_rows(): pl.pallas_call(functools.partial(pick_kernel, whole=whole, tucked=tucked,...]
  transfers between devices with their start and end apart: 3 -> 3, of which waited for: 2 -> 2; matrix products, arithmetic and copies ran while one was open for 6% -> 6% of each run, Pallas kernels for 11% -> 7%
where the time goes in v3:
time: 83.1 us; the launch traced here: 82.5 us
  Pallas kernels  26 us (31%)
  waiting for transfers between devices  18.1 us (22%)
  blocking collectives  14.8 us (18%)
  starting transfers between devices  13.2 us (16%)
  local copies, waits for them, and re-layouts  8.04 us (10%)
  other arithmetic  2.15 us (3%)
    ppermute x1, waiting for transfers between devices, local(): lax.ppermute(own, 'node', [(i, (i + half) % groups) for i in range(groups)])  16.7 us
    pallas_call x1, Pallas kernels, attend(): pl.pallas_call(functools.partial(attend_kernel, whole=whole, tucked=tucke...  14.3 us
    pallas_call x2, Pallas kernels, pick_rows(): pl.pallas_call(functools.partial(pick_kernel, whole=whole, tucked=tucked,...  11.7 us
    all_to_all x2, starting transfers between devices, within(): lax.all_to_all(values, 'node', split_axis=0, concat_axis=0, axis_index_gr...  10.5 us
    all_to_all x1, blocking collectives, within(): lax.all_to_all(values, 'node', split_axis=0, concat_axis=0, axis_index_gr...  9.81 us
    all_gather x1, blocking collectives, shared_weights(): both = lax.all_gather(mine, 'head', axis=0, tiled=False)  4.97 us
    unnamed x28, local copies, waits for them, and re-layouts  4.11 us
    ppermute x1, starting transfers between devices, local(): lax.ppermute(own, 'node', [(i, (i + half) % groups) for i in range(groups)])  2.65 us
  transfers between devices with their start and end apart: 3, of which 2 were waited for; matrix products, arithmetic and copies ran while one was open for 6% of the time, Pallas kernels for 7%

profile of v3, /device:TPU:0, one launch (start us, length us, event | category | flops | bytes accessed | tf_op | source)
XLA Modules:
  0.0 82.5 jit_solution(12809209044151698511)
XLA Ops:
  0.0 0.8 copy-done.4
  0.8 0.2 rev.3
  1.1 9.8 %all_to_all.15 = s32[8,8,128]{2,1,0:T(8,128)S(1)} all-to-all(s32[8,8,128]{2,1,0:T(8,128)S(1)} %reshape.56), channel_id=1, replica_groups={{0,2,4,6,8,10,12,14},{16,18,20,22,24,26,28,30},{1,3,5,7,9,11,13,15},{17..., dimensions={0} | all-to-all | bytes 65536 | tf_op jit(solution)/shard_map/all_to_all | solution.py:283
  10.9 0.6 fusion.17
  11.6 5.9 %pick.2 = bf16[8,416,128]{2,1,0:T(8,128)(2,1)} custom-call(s32[4096]{0:T(1024)} %bitcast.40, bf16[100,2048]{1,0:T(8,128)(2,1)} %bitcast.31), custom_call_target="tpu_custom_call" | custom-call | tf_op jit(solution)/shard_map/pick/pallas_call | solution.py:81
  17.4 3.7 %all-to-all-start.1 = ((bf16[8,416,128]{2,1,0:T(8,128)(2,1)}), bf16[8,416,128]{2,1,0:T(8,128)(2,1)S(1)}, u32[]{:S(2)}, u32[]{:S(2)}) async-start(bf16[8,416,128]{2,1,0:T(8,128)(2,1)} %pick.2), calls=%async_computation.1 | async-start | bytes 1703936 | tf_op jit(solution)/shard_map/all_to_all | solution.py:283
  21.1 2.6 %collective-permute-start = (bf16[100,2048]{1,0:T(8,128)(2,1)S(1)}, bf16[100,2048]{1,0:T(8,128)(2,1)S(1)}, u32[]{:S(2)}, u32[]{:S(2)}) collective-permute-start(bf16[100,2048]{1,0:T(8,128)(2,1)S(1)} %bitcast.32), channel_id=1, source_target_pairs={{0,16},{2,18},{4,20},{6,22},{8,24},{10,26},{12,28},{14,30},{16,0},... | collective-permute-start | bytes 1228808 | tf_op jit(solution)/shard_map/ppermute | solution.py:280
  23.8 16.7 %collective-permute-done.features = bf16[100,2048]{1,0:T(8,128)(2,1)S(1)} collective-permute-done((bf16[100,2048]{1,0:T(8,128)(2,1)S(1)}, bf16[100,2048]{1,0:T(8,128)(2,1)S(1)}, u32[]{:S(2)}, u32[]{:S(2)}) %collective-permute-start) | collective-permute-done | bytes 409632 | tf_op jit(solution)/shard_map/ppermute | solution.py:280
  40.5 0.7 copy-done.3
  41.2 5.8 %pick.3 = bf16[8,416,128]{2,1,0:T(8,128)(2,1)} custom-call(s32[4096]{0:T(1024)} %bitcast.39, bf16[100,2048]{1,0:T(8,128)(2,1)} %copy-done.3), custom_call_target="tpu_custom_call" | custom-call | tf_op jit(solution)/shard_map/pick/pallas_call | solution.py:81
  47.1 0.9 %copy-done = bf16[8,416,128]{2,1,0:T(8,128)(2,1)} copy-done((bf16[8,416,128]{2,1,0:T(8,128)(2,1)}, bf16[8,416,128]{2,1,0:T(8,128)(2,1)S(1)}, u32[]{:S(2)}) %copy-start) | copy-done | bytes 851992
  48.0 6.8 %all-to-all-start.2 = ((bf16[8,416,128]{2,1,0:T(8,128)(2,1)}), bf16[8,416,128]{2,1,0:T(8,128)(2,1)S(1)}, u32[]{:S(2)}, u32[]{:S(2)}) async-start(bf16[8,416,128]{2,1,0:T(8,128)(2,1)} %pick.3), calls=%async_computation.2 | async-start | bytes 1703936 | tf_op jit(solution)/shard_map/all_to_all | solution.py:283
  55.0 0.7 reshape.54.slots
  55.7 0.1 reshape.58
  56.0 0.6 copy-done.8
  56.9 5.0 %all-gather.1 = bf16[2,106,256]{2,1,0:T(8,128)(2,1)S(1)} all-gather(bf16[1,106,256]{2,1,0:T(8,128)(2,1)S(1)} %bitcast.36), channel_id=2, replica_groups=mesh['node'=16,'head'=2] {'head'}, dimensions={0}, use_global_device_ids=true | all-gather | bytes 162816 | tf_op jit(solution)/shard_map/all_gather | solution.py:249
  62.1 0.1 pad.5
  62.2 0.7 pad.4.weight
  62.9 0.8 copy.19.counts
  63.8 0.7 fusion.10.spread
  64.4 1.4 %fusion.9.scores = bf16[512,128]{1,0:T(8,128)(2,1)} fusion(s32[512]{0:T(512)S(1)} %get-tuple-element.19, s32[512]{0:T(512)S(1)} %get-tuple-element.20, pred[512]{0:T(512)(128)(4,1)S(1)} %fusion.16, bf16[512]{0:T(512)(128)(2,1)S(1)} %bitcast.46, bf16[512]{0:T(512)(128)(2,1)S(1)} %bitcast.45, bf16[512]{0:T(512)(128)(2,1)S(1)} %bitcast.44, ...), kind=kLoop, calls=%fused_computation.16 | loop fusion | flops 1179648 | bytes 141824 | tf_op jit(solution)/shard_map/jit(_where)/select_n | solution.py:256
  65.8 1.4 %all-to-all-done.2.far = bf16[8,416,128]{2,1,0:T(8,128)(2,1)S(1)} async-done(((bf16[8,416,128]{2,1,0:T(8,128)(2,1)}), bf16[8,416,128]{2,1,0:T(8,128)(2,1)S(1)}, u32[]{:S(2)}, u32[]{:S(2)}) %all-to-all-start.2) | async-done | bytes 852000 | tf_op jit(solution)/shard_map/all_to_all | solution.py:283
  67.3 0.9 %copy-done.1 = bf16[8,416,128]{2,1,0:T(8,128)(2,1)} copy-done((bf16[8,416,128]{2,1,0:T(8,128)(2,1)}, bf16[8,416,128]{2,1,0:T(8,128)(2,1)S(1)}, u32[]{:S(2)}) %copy-start.1) | copy-done | bytes 851992
  68.2 14.3 %attend.1 = bf16[256,512]{1,0:T(8,128)(2,1)} custom-call(s32[4096]{0:T(1024)} %reshape.54.slots, bf16[8,416,128]{2,1,0:T(8,128)(2,1)} %copy-done, bf16[8,416,128]{2,1,0:T(8,128)(2,1)} %copy-done.1, bf16[128,512]{1,0:T(8,128)(2,1)} %pad.4.weight, bf16[512,128]{1,0:T(8,128)(2,1)} %fusion.9.scores, bf16[128,512]{1,0:T(8,128)(2,1)} %fusion.10.spread, ...), custom_call_target="tpu_custom_call" | custom-call | tf_op jit(solution)/shard_map/attend/pallas_call | solution.py:206
  (44 shorter events, 1.0 us)
Async XLA Ops:
  0.0 0.8 copy-start.4
  17.4 3.7 %copy-start.2 = (bf16[2048,100]{0,1:T(8,128)(2,1)S(1)}, bf16[2048,100]{0,1:T(8,128)(2,1)}, u32[]{:S(2)}) copy-start(bf16[2048,100]{0,1:T(8,128)(2,1)} %param.8) | copy-start | bytes 1228804
  17.4 29.7 %all-to-all-start.1 = ((bf16[8,416,128]{2,1,0:T(8,128)(2,1)}), bf16[8,416,128]{2,1,0:T(8,128)(2,1)S(1)}, u32[]{:S(2)}, u32[]{:S(2)}) async-start(bf16[8,416,128]{2,1,0:T(8,128)(2,1)} %pick.2), calls=%async_computation.1 | async-start | bytes 1703936 | tf_op jit(solution)/shard_map/all_to_all | solution.py:283
  21.1 19.3 %collective-permute-start = (bf16[100,2048]{1,0:T(8,128)(2,1)S(1)}, bf16[100,2048]{1,0:T(8,128)(2,1)S(1)}, u32[]{:S(2)}, u32[]{:S(2)}) collective-permute-start(bf16[100,2048]{1,0:T(8,128)(2,1)S(1)} %bitcast.32), channel_id=1, source_target_pairs={{0,16},{2,18},{4,20},{6,22},{8,24},{10,26},{12,28},{14,30},{16,0},... | collective-permute-start | bytes 1228808 | tf_op jit(solution)/shard_map/ppermute | solution.py:280
  40.5 0.7 copy-start.3
  47.1 7.8 %copy-start.6 = (s32[512,16]{0,1:T(8,128)S(1)}, s32[512,16]{0,1:T(8,128)}, u32[]{:S(2)}) copy-start(s32[512,16]{0,1:T(8,128)} %param.13) | copy-start | bytes 98308
  47.1 0.9 %copy-start = (bf16[8,416,128]{2,1,0:T(8,128)(2,1)}, bf16[8,416,128]{2,1,0:T(8,128)(2,1)S(1)}, u32[]{:S(2)}) copy-start(bf16[8,416,128]{2,1,0:T(8,128)(2,1)S(1)} %all-to-all-done.1.near) | copy-start | bytes 2555908
  48.0 19.2 %all-to-all-start.2 = ((bf16[8,416,128]{2,1,0:T(8,128)(2,1)}), bf16[8,416,128]{2,1,0:T(8,128)(2,1)S(1)}, u32[]{:S(2)}, u32[]{:S(2)}) async-start(bf16[8,416,128]{2,1,0:T(8,128)(2,1)} %pick.3), calls=%async_computation.2 | async-start | bytes 1703936 | tf_op jit(solution)/shard_map/all_to_all | solution.py:283
  55.0 0.7 copy-start.7
  55.0 1.8 %copy-start.5 = (bf16[100,256]{1,0:T(8,128)(2,1)S(1)}, bf16[100,256]{1,0:T(8,128)(2,1)}, u32[]{:S(2)}) copy-start(bf16[100,256]{1,0:T(8,128)(2,1)} %param.9) | copy-start | bytes 153604
  55.9 0.7 copy-start.8
  62.2 0.7 copy-start.9
  67.2 0.9 %copy-start.1 = (bf16[8,416,128]{2,1,0:T(8,128)(2,1)}, bf16[8,416,128]{2,1,0:T(8,128)(2,1)S(1)}, u32[]{:S(2)}) copy-start(bf16[8,416,128]{2,1,0:T(8,128)(2,1)S(1)} %all-to-all-done.2.far) | copy-start | bytes 2555908

commit v4 on v3

v4 whole, which is shorter than its diff:
```python
import functools
import math

import jax
import jax.numpy as jnp
from jax import lax
from jax.experimental import pallas as pl
from jax.experimental.pallas import tpu as pltpu
from jax.sharding import PartitionSpec as P


LANES = 128
DEPTH = 4


def spare_split(capacity, feat):
    tucked = capacity * 3 // 16
    piece = -(-feat // 4)
    if tucked % 8 or (capacity - tucked) % 16 or feat + piece > LANES:
        return capacity, 0, piece
    return capacity - tucked, tucked, piece


def copy_rows(index, table, out, count, start=0):
    for place in range(count):
        out[place : place + 1, :] = table[pl.ds(index[start + place], 1), :]


def in_turn(lists, total, count, buffers, sems, setup, work):
    depth = len(buffers)

    def fetch(number, turn):
        source = lists.at[pl.ds(number * count, count)]
        return pltpu.make_async_copy(source, buffers[turn], sems.at[turn])

    for turn in range(depth):
        fetch(turn, turn).start()

    setup()

    @pl.loop(0, total // depth)
    def _(group):
        for turn in range(depth):
            number = group * depth + turn
            fetch(number, turn).wait()
            work(number, buffers[turn])

            @pl.when(number + depth < total)
            def _():
                fetch(number + depth, turn).start()


def pick_kernel(wanted, features, packed, table, rows, *lists, whole, tucked, piece):
    feat, nodes = features.shape
    capacity = whole + tucked

    def setup():
        table[...] = jnp.zeros(table.shape, jnp.float32)
        for first in range(0, nodes, LANES):
            last = min(first + LANES, nodes)
            table[first:last, :feat] = features[:, first:last].astype(jnp.float32).T

    tiles = lists[0].shape[0] // capacity

    def work(number, buffer):
        for tile in range(tiles):
            one_peer(number * tiles + tile, buffer, tile * capacity)

    def one_peer(peer, buffer, start):
        copy_rows(buffer, table, rows, capacity, start)
        if tucked:
            lane = lax.broadcasted_iota(jnp.int32, (tucked, LANES), 1)
            spare = (lane >= feat) & (lane < feat + piece)
            extra = rows[whole:, :]
            for part in range(4):
                first = part * tucked
                moved = pltpu.roll(extra, feat - part * piece, axis=1)
                rows[first : first + tucked, :] = jnp.where(
                    spare, moved, rows[first : first + tucked, :]
                )
        packed[peer] = rows[:whole, :].astype(packed.dtype)

    in_turn(wanted, packed.shape[0] // tiles, tiles * capacity, lists[:-1], lists[-1], setup, work)


def pick_rows(wanted, features, peers):
    capacity = wanted.shape[0] // peers
    feat, nodes = features.shape
    whole, tucked, piece = spare_split(capacity, feat)
    tiles = math.gcd(peers, max(1, LANES // capacity))
    depth = math.gcd(DEPTH, peers // tiles)
    return pl.pallas_call(
        functools.partial(pick_kernel, whole=whole, tucked=tucked, piece=piece),
        in_specs=[
            pl.BlockSpec(memory_space=pl.ANY),
            pl.BlockSpec(memory_space=pltpu.VMEM),
        ],
        out_specs=pl.BlockSpec(memory_space=pltpu.VMEM),
        scratch_shapes=[
            pltpu.VMEM((nodes, LANES), jnp.float32),
            pltpu.VMEM((capacity, LANES), jnp.float32),
        ]
        + [pltpu.SMEM((tiles * capacity,), jnp.int32)] * depth
        + [pltpu.SemaphoreType.DMA((depth,))],
        out_shape=jax.ShapeDtypeStruct((peers, whole, LANES), features.dtype),
        name="pick",
    )(wanted, features)


def unpack(packed, table, start, whole, capacity, piece, feat):
    tucked = capacity - whole

    @pl.loop(0, packed.shape[0])
    def _(owner):
        base = pl.multiple_of(start + owner * capacity, 8)
        sent = packed[owner].astype(jnp.float32)
        table[pl.ds(base, whole), :] = sent
        if tucked:
            lane = lax.broadcasted_iota(jnp.int32, (tucked, LANES), 1)
            extra = jnp.zeros((tucked, LANES), jnp.float32)
            for part in range(4):
                moved = pltpu.roll(
                    sent[part * tucked : (part + 1) * tucked],
                    (LANES - feat + part * piece) % LANES,
                    axis=1,
                )
                extra = jnp.where(
                    (lane >= part * piece) & (lane < (part + 1) * piece), moved, extra
                )
            table[pl.ds(base + whole, tucked), :] = extra


def project(rows, weight, scores, heads):
    zvals = jnp.dot(
        rows[...].astype(jnp.bfloat16), weight[...], preferred_element_type=jnp.float32
    ).astype(jnp.bfloat16)
    parts = lax.dot_general(
        zvals, scores[...], (((1,), (1,)), ((), ())), preferred_element_type=jnp.float32
    )
    sums = (
        parts
        + pltpu.roll(parts, LANES - heads, axis=1)
        + pltpu.roll(parts, LANES - 2 * heads, axis=1)
    )
    return zvals, sums


def combine(zvals, sums, live, spread, heads, block, slot_total):
    dst = pltpu.roll(sums[:block, :], LANES - 3 * heads, axis=1)
    logits = []
    for slot in range(slot_total):
        logit = sums[slot * block : (slot + 1) * block, :] + dst
        logit = jnp.maximum(logit, 0.2 * logit)
        logits.append(jnp.where(live > slot, logit, -1e30))
    peak = functools.reduce(jnp.maximum, logits)
    shares = [jnp.exp(logit - peak) for logit in logits]
    scale = 1.0 / functools.reduce(jnp.add, shares)
    summed = None
    for slot in range(slot_total):
        alpha = (shares[slot] * scale).astype(jnp.bfloat16)
        wide = jnp.dot(alpha, spread[...], preferred_element_type=jnp.float32)
        term = wide * zvals[slot * block : (slot + 1) * block, :].astype(jnp.float32)
        summed = term if summed is None else summed + term
    low = jnp.minimum(summed, 0.0)
    series = low * (1.0 + low * (0.5 + low * (1.0 / 6.0)))
    below = jnp.where(low > -0.01, series, jnp.exp(low) - 1.0)
    return jnp.where(summed > 0, summed, below)


def attend_kernel(
    *refs, near_total, whole, part_whole, capacity, part, piece, feat, heads, block, slot_total
):
    slots, shared, counts, out_weight, far = refs[:5]
    nears = refs[5 : 5 + near_total]
    (
        out, table, rows_even, rows_odd, z_even, z_odd, sums_even, sums_odd, hidden,
        raw, weight, scores, spread, live, even, odd, sems,
    ) = refs[5 + near_total :]
    dst_rows, width = hidden.shape
    blocks = dst_rows // block
    count = block * slot_total
    rows, z, sums = (rows_even, rows_odd), (z_even, z_odd), (sums_even, sums_odd)
    lists = (even, odd)

    def fetch(number, turn):
        source = slots.at[pl.ds(jnp.minimum(number, blocks - 1) * count, count)]
        return pltpu.make_async_copy(source, lists[turn], sems.at[turn])

    fetch(0, 0).start()
    fetch(1, 1).start()

    raw[...] = jnp.zeros(raw.shape, jnp.float32)
    scores[...] = jnp.zeros(scores.shape, scores.dtype)
    side_width = shared.shape[2]
    for side in range(shared.shape[0]):
        raw[: shared.shape[1], side * side_width : (side + 1) * side_width] = shared[
            side
        ].astype(jnp.float32)
    row = lax.broadcasted_iota(jnp.int32, (LANES, width), 0)
    owner = lax.broadcasted_iota(jnp.int32, (LANES, width), 1) // (width // heads)
    weight[...] = jnp.where(row < feat, raw[...], 0.0).astype(jnp.bfloat16)
    spread[...] = jnp.where(row == owner, 1.0, 0.0).astype(jnp.bfloat16)
    lines = [
        jnp.where(
            row[:heads] == owner[:heads],
            jnp.broadcast_to(raw[feat + rank : feat + rank + 1, :], (heads, width)),
            0.0,
        )
        for rank in range(6)
    ]
    scores[: 6 * heads, :] = jnp.concatenate(lines, axis=0).astype(jnp.bfloat16)
    live[...] = jnp.broadcast_to(counts[...], (LANES, dst_rows)).T

    owners = far.shape[0]
    base = 0
    for near in nears:
        unpack(near, table, base, part_whole, part, piece, feat)
        base += owners * part
    unpack(far, table, base, whole, capacity, piece, feat)

    def first_stage(turn):
        zvals, scored = project(rows[turn], weight, scores, heads)
        z[turn][...] = zvals
        sums[turn][...] = scored

    fetch(0, 0).wait()
    copy_rows(even, table, rows_even, count)
    fetch(2, 0).start()
    fetch(1, 1).wait()
    copy_rows(odd, table, rows_odd, count)
    fetch(3, 1).start()
    first_stage(0)

    @pl.loop(0, blocks // 2)
    def _(pair):
        for turn in range(2):
            number = 2 * pair + turn
            first = pl.multiple_of(number * block, 8)
            fetch(number + 2, turn).wait()
            copy_rows(lists[turn], table, rows[turn], count)
            first_stage(1 - turn)
            hidden[pl.ds(first, block), :] = combine(
                z[turn], sums[turn], live[pl.ds(first, block), :], spread, heads, block, slot_total
            )
            fetch(number + 4, turn).start()

    fetch(0, 0).wait()
    fetch(0, 1).wait()
    out[...] = jnp.dot(
        hidden[...].astype(jnp.bfloat16), out_weight[...], preferred_element_type=jnp.float32
    ).astype(out.dtype)


def attend(slots, shared, counts, out_weight, far, nears, capacity, part, feat, heads, block):
    whole, _, piece = spare_split(capacity, feat)
    part_whole, _, _ = spare_split(part, feat)
    dst_rows = counts.shape[1]
    slot_total = slots.shape[0] // dst_rows
    width = out_weight.shape[0]
    count = block * slot_total
    return pl.pallas_call(
        functools.partial(
            attend_kernel,
            near_total=len(nears),
            whole=whole,
            part_whole=part_whole,
            capacity=capacity,
            part=part,
            piece=piece,
            feat=feat,
            heads=heads,
            block=block,
            slot_total=slot_total,
        ),
        in_specs=[pl.BlockSpec(memory_space=pl.ANY)]
        + [pl.BlockSpec(memory_space=pltpu.VMEM)] * (4 + len(nears)),
        out_specs=pl.BlockSpec(memory_space=pltpu.VMEM),
        scratch_shapes=[
            pltpu.VMEM((2 * far.shape[0] * capacity, LANES), jnp.float32),
            pltpu.VMEM((count, LANES), jnp.float32),
            pltpu.VMEM((count, LANES), jnp.float32),
            pltpu.VMEM((count, width), jnp.bfloat16),
            pltpu.VMEM((count, width), jnp.bfloat16),
            pltpu.VMEM((count, LANES), jnp.float32),
            pltpu.VMEM((count, LANES), jnp.float32),
            pltpu.VMEM((dst_rows, width), jnp.float32),
            pltpu.VMEM((LANES, width), jnp.float32),
            pltpu.VMEM((LANES, width), jnp.bfloat16),
            pltpu.VMEM((LANES, width), jnp.bfloat16),
            pltpu.VMEM((LANES, width), jnp.bfloat16),
            pltpu.VMEM((dst_rows, LANES), jnp.float32),
            pltpu.SMEM((count,), jnp.int32),
            pltpu.SMEM((count,), jnp.int32),
            pltpu.SemaphoreType.DMA((2,)),
        ],
        out_shape=jax.ShapeDtypeStruct((dst_rows, out_weight.shape[1]), jnp.bfloat16),
        name="attend",
    )(slots, shared, counts, out_weight, far, *nears)


def three_pieces(values):
    high = lax.reduce_precision(values, 8, 7)
    rest = values - high
    middle = lax.reduce_precision(rest, 8, 7)
    return [piece.astype(jnp.bfloat16) for piece in (high, middle, rest - middle)]


def shared_weights(proj_weight, score_src, score_dst):
    pieces = [
        piece.reshape(1, -1) for score in (score_src, score_dst) for piece in three_pieces(score)
    ]
    mine = jnp.concatenate([proj_weight] + pieces, axis=0)
    return lax.all_gather(mine, "head", axis=0, tiled=False)


def local(
    features, proj_weight, score_src, score_dst, request_rows, slot_index, slot_count, out_weight
):
    groups = lax.axis_size("node")
    half = groups // 2
    upper = lax.axis_index("node") // half
    halves = [list(range(half)), list(range(half, groups))]
    sides = lax.axis_size("head")
    side = lax.axis_index("head")
    capacity = request_rows.shape[2]
    feat = features.shape[1]
    slot_total = slot_index.shape[1]
    dst_rows = slot_index.shape[0] // sides
    block = min(32, dst_rows // 2)

    own = features.T
    across = lax.ppermute(own, "node", [(i, (i + half) % groups) for i in range(groups)])

    def within(values):
        return lax.all_to_all(
            values, "node", split_axis=0, concat_axis=0, axis_index_groups=halves, tiled=True
        )

    part = capacity // sides
    requests = request_rows.reshape(2, half, capacity)
    requests = jnp.where(upper == 0, requests, requests[::-1])
    near_asked = lax.dynamic_slice_in_dim(requests[0], side * part, part, 1)
    asked = jnp.concatenate([near_asked, requests[1]], axis=1)
    lanes = math.gcd(asked.shape[1], LANES)
    wanted = within(asked.reshape(half, asked.shape[1] // lanes, lanes))
    wanted = wanted.reshape(asked.shape)

    picked = pick_rows(wanted[:, :part].reshape(-1), own, half)
    nears = [within(picked)]
    far = within(pick_rows(wanted[:, part:].reshape(-1), across, half))
    for step in range(1, sides):
        ring = [(i, (i + step) % sides) for i in range(sides)]
        nears.append(lax.ppermute(nears[0], "head", ring))

    shared = shared_weights(proj_weight, score_src, score_dst)
    heads = score_src.shape[0] * sides
    slots = lax.dynamic_slice_in_dim(slot_index, side * dst_rows, dst_rows, 0)
    owner, place = slots // capacity, slots % capacity
    peer = owner % half
    turn = (side - place // part) % sides
    slots = jnp.where(
        owner // half == upper,
        (turn * half + peer) * part + place % part,
        (half + peer) * capacity + place,
    )
    slots = jnp.transpose(
        slots.reshape(dst_rows // block, block, slot_total), (0, 2, 1)
    ).reshape(-1)
    counts = lax.dynamic_slice_in_dim(slot_count, side * dst_rows, dst_rows, 0)
    counts = counts.astype(jnp.float32)[None, :]
    return attend(
        slots, shared, counts, out_weight, far, nears, capacity, part, feat, heads, block
    )


def solution(mesh):
    in_specs = (
        P("node", None),
        P(None, "head"),
        P("head", None),
        P("head", None),
        P("node", None, None),
        P("node", None),
        P("node"),
        P(),
    )
    out_specs = P(("node", "head"), None)
    return jax.shard_map(local, mesh=mesh, in_specs=in_specs, out_specs=out_specs, check_vma=False)
```

time: 83.1 us -> 81.5 us (0.981)
  blocking collectives: 14.8 us -> 19.7 us
  local copies, waits for them, and re-layouts: 8.04 us -> 5.75 us
  Pallas kernels: 26 us -> 24.1 us
  starting transfers between devices: 13.2 us -> 11.4 us
  other arithmetic: 2.15 us -> 0.73 us
    all_gather x1, blocking collectives: 4.97 us -> 9.89 us  [shared_weights(): return lax.all_gather(mine, 'head', axis=0, tiled=False)]
    all_to_all x2, starting transfers between devices: 10.5 us -> 7.17 us  [within(): lax.all_to_all(values, 'node', split_axis=0, concat_axis=0, axis_index_gr...]
    ppermute x1, waiting for transfers between devices: 16.7 us -> 18.9 us  [local(): lax.ppermute(own, 'node', [(i, (i + half) % groups) for i in range(groups)])]
    pallas_call x2, Pallas kernels: 11.7 us -> 9.94 us  [pick_rows(): pl.pallas_call(functools.partial(pick_kernel, whole=whole, tucked=tucked,...]
    ppermute x0 -> x1, starting transfers between devices: none -> 1.59 us  [local(): nears.append(lax.ppermute(nears[0], 'head', ring))]
    all_to_all x2, waiting for transfers between devices: 1.4 us -> 0.01 us  [within(): lax.all_to_all(values, 'node', split_axis=0, concat_axis=0, axis_index_gr...]
    select_n x2, other arithmetic: 1.41 us -> 0.07 us  [the longest x1 0.06 us: local(): jnp.where(owner // half == upper, (turn * half + peer) * part + place % p...]
    unnamed x28 -> x27, local copies, waits for them, and re-layouts: 4.11 us -> 4.4 us
  transfers between devices with their start and end apart: 3 -> 4, of which waited for: 2 -> 1; matrix products, arithmetic and copies ran while one was open for 6% -> 3% of each run, Pallas kernels for 7% -> 7%
where the time goes in v4:
time: 81.5 us; the launch traced here: 80.8 us
  Pallas kernels  24.1 us (30%)
  blocking collectives  19.7 us (24%)
  waiting for transfers between devices  18.9 us (23%)
  starting transfers between devices  11.4 us (14%)
  local copies, waits for them, and re-layouts  5.75 us (7%)
    ppermute x1, waiting for transfers between devices, local(): lax.ppermute(own, 'node', [(i, (i + half) % groups) for i in range(groups)])  18.9 us
    pallas_call x1, Pallas kernels, attend(): pl.pallas_call(functools.partial(attend_kernel, near_total=len(nears), wh...  14.2 us
    pallas_call x2, Pallas kernels, pick_rows(): pl.pallas_call(functools.partial(pick_kernel, whole=whole, tucked=tucked,...  9.94 us
    all_gather x1, blocking collectives, shared_weights(): return lax.all_gather(mine, 'head', axis=0, tiled=False)  9.89 us
    all_to_all x1, blocking collectives, within(): lax.all_to_all(values, 'node', split_axis=0, concat_axis=0, axis_index_gr...  9.81 us
    all_to_all x2, starting transfers between devices, within(): lax.all_to_all(values, 'node', split_axis=0, concat_axis=0, axis_index_gr...  7.17 us
    unnamed x27, local copies, waits for them, and re-layouts  4.4 us
    ppermute x1, starting transfers between devices, local(): lax.ppermute(own, 'node', [(i, (i + half) % groups) for i in range(groups)])  2.65 us
  transfers between devices with their start and end apart: 4, of which 1 were waited for; matrix products, arithmetic and copies ran while one was open for 3% of the time, Pallas kernels for 7%

profile of v4, /device:TPU:0, one launch (start us, length us, event | category | flops | bytes accessed | tf_op | source)
XLA Modules:
  0.0 80.8 jit_solution(6395392416733803384)
XLA Ops:
  0.0 0.8 copy-done.6
  0.8 9.8 %all_to_all.15 = s32[8,6,128]{2,1,0:T(8,128)S(1)} all-to-all(s32[8,6,128]{2,1,0:T(8,128)S(1)} %copy.12), channel_id=1, replica_groups={{0,2,4,6,8,10,12,14},{16,18,20,22,24,26,28,30},{1,3,5,7,9,11,13,15},{17..., dimensions={0} | all-to-all | bytes 49152 | tf_op jit(solution)/shard_map/all_to_all | solution.py:335
  10.6 0.6 copy.15
  11.2 4.1 %pick.3 = bf16[8,208,128]{2,1,0:T(8,128)(2,1)} custom-call(s32[2048]{0:T(1024)} %bitcast.33, bf16[100,2048]{1,0:T(8,128)(2,1)} %bitcast.25), custom_call_target="tpu_custom_call" | custom-call | tf_op jit(solution)/shard_map/pick/pallas_call | solution.py:92
  15.4 3.6 %all-to-all-start.2 = ((bf16[8,208,128]{2,1,0:T(8,128)(2,1)}), bf16[8,208,128]{2,1,0:T(8,128)(2,1)S(1)}, u32[]{:S(2)}, u32[]{:S(2)}) async-start(bf16[8,208,128]{2,1,0:T(8,128)(2,1)} %pick.3), calls=%async_computation.2 | async-start | bytes 851968 | tf_op jit(solution)/shard_map/all_to_all | solution.py:335
  19.0 2.7 %collective-permute-start = (bf16[100,2048]{1,0:T(8,128)(2,1)S(1)}, bf16[100,2048]{1,0:T(8,128)(2,1)S(1)}, u32[]{:S(2)}, u32[]{:S(2)}) collective-permute-start(bf16[100,2048]{1,0:T(8,128)(2,1)S(1)} %bitcast.26), channel_id=1, source_target_pairs={{0,16},{2,18},{4,20},{6,22},{8,24},{10,26},{12,28},{14,30},{16,0},... | collective-permute-start | bytes 1228808 | tf_op jit(solution)/shard_map/ppermute | solution.py:332
  21.6 0.6 copy.14
  22.3 18.9 %collective-permute-done.features = bf16[100,2048]{1,0:T(8,128)(2,1)S(1)} collective-permute-done((bf16[100,2048]{1,0:T(8,128)(2,1)S(1)}, bf16[100,2048]{1,0:T(8,128)(2,1)S(1)}, u32[]{:S(2)}, u32[]{:S(2)}) %collective-permute-start) | collective-permute-done | bytes 409632 | tf_op jit(solution)/shard_map/ppermute | solution.py:332
  41.2 0.8 copy-done.3
  42.0 5.8 %pick.2 = bf16[8,416,128]{2,1,0:T(8,128)(2,1)} custom-call(s32[4096]{0:T(1024)} %bitcast.32, bf16[100,2048]{1,0:T(8,128)(2,1)} %copy-done.3), custom_call_target="tpu_custom_call" | custom-call | tf_op jit(solution)/shard_map/pick/pallas_call | solution.py:92
  47.8 3.6 %all-to-all-start.1 = ((bf16[8,416,128]{2,1,0:T(8,128)(2,1)}), bf16[8,416,128]{2,1,0:T(8,128)(2,1)S(1)}, u32[]{:S(2)}, u32[]{:S(2)}) async-start(bf16[8,416,128]{2,1,0:T(8,128)(2,1)} %pick.2), calls=%async_computation.1 | async-start | bytes 1703936 | tf_op jit(solution)/shard_map/all_to_all | solution.py:335
  51.4 1.6 %collective-permute-start.1 = (bf16[8,208,128]{2,1,0:T(8,128)(2,1)S(1)}, bf16[8,208,128]{2,1,0:T(8,128)(2,1)S(1)}, u32[]{:S(2)}, u32[]{:S(2)}) collective-permute-start(bf16[8,208,128]{2,1,0:T(8,128)(2,1)S(1)} %all-to-all-done.2.refs_5_), channel_id=1, source_target_pairs={{0,1},{1,0},{2,3},{3,2},{4,5},{5,4},{6,7},{7,6},{8,9},{9,8},{10,11... | collective-permute-start | bytes 1277960 | tf_op jit(solution)/shard_map/ppermute | solution.py:353
  53.2 0.7 reshape.41.refs_0_
  53.9 0.1 reshape.42
  54.1 0.1 reshape.44
  54.1 0.6 copy-done.9
  54.8 0.1 reshape.45
  54.8 0.1 reshape.46
  54.9 0.1 reshape.47
  55.1 9.9 %all-gather.1.refs_1_ = bf16[2,106,256]{2,1,0:T(8,128)(2,1)} all-gather(bf16[1,106,256]{2,1,0:T(8,128)(2,1)S(1)} %bitcast.28), channel_id=2, replica_groups=mesh['node'=16,'head'=2] {'head'}, dimensions={0}, use_global_device_ids=true | all-gather | bytes 162816 | tf_op jit(solution)/shard_map/all_gather | solution.py:313
  65.0 0.6 dynamic-slice_convert_fusion
  65.6 0.7 copy-done.2
  66.4 0.3 copy-done
  66.6 14.2 %attend.1 = bf16[256,512]{1,0:T(8,128)(2,1)} custom-call(s32[4096]{0:T(1024)} %reshape.41.refs_0_, bf16[2,106,256]{2,1,0:T(8,128)(2,1)} %all-gather.1.refs_1_, f32[1,256]{1,0:T(1,128)} %bitcast.35, bf16[512,512]{1,0:T(8,128)(2,1)} %refs_3_.1, bf16[8,416,128]{2,1,0:T(8,128)(2,1)} %copy-done, bf16[8,208,128]{2,1,0:T(8,128)(2,1)} %copy-done.1, ...), custom_call_target="tpu_custom_call" | custom-call | tf_op jit(solution)/shard_map/attend/pallas_call | solution.py:261
  (35 shorter events, 0.4 us)
Async XLA Ops:
  0.0 0.8 copy-start.6
  15.4 3.6 %copy-start.4 = (bf16[2048,100]{0,1:T(8,128)(2,1)S(1)}, bf16[2048,100]{0,1:T(8,128)(2,1)}, u32[]{:S(2)}) copy-start(bf16[2048,100]{0,1:T(8,128)(2,1)} %param.8) | copy-start | bytes 1228804
  15.4 32.4 %all-to-all-start.2 = ((bf16[8,208,128]{2,1,0:T(8,128)(2,1)}), bf16[8,208,128]{2,1,0:T(8,128)(2,1)S(1)}, u32[]{:S(2)}, u32[]{:S(2)}) async-start(bf16[8,208,128]{2,1,0:T(8,128)(2,1)} %pick.3), calls=%async_computation.2 | async-start | bytes 851968 | tf_op jit(solution)/shard_map/all_to_all | solution.py:335
  19.0 22.2 %collective-permute-start = (bf16[100,2048]{1,0:T(8,128)(2,1)S(1)}, bf16[100,2048]{1,0:T(8,128)(2,1)S(1)}, u32[]{:S(2)}, u32[]{:S(2)}) collective-permute-start(bf16[100,2048]{1,0:T(8,128)(2,1)S(1)} %bitcast.26), channel_id=1, source_target_pairs={{0,16},{2,18},{4,20},{6,22},{8,24},{10,26},{12,28},{14,30},{16,0},... | collective-permute-start | bytes 1228808 | tf_op jit(solution)/shard_map/ppermute | solution.py:332
  41.2 0.8 copy-start.3
  47.8 3.6 %copy-start.8 = (f32[4,64]{1,0:T(4,128)S(1)}, f32[4,64]{1,0:T(4,128)}, u32[]{:S(2)}) copy-start(f32[4,64]{1,0:T(4,128)} %param.10) | copy-start | bytes 3076
  47.8 5.2 %copy-start.7 = (s32[512,16]{0,1:T(8,128)S(1)}, s32[512,16]{0,1:T(8,128)}, u32[]{:S(2)}) copy-start(s32[512,16]{0,1:T(8,128)} %param.13) | copy-start | bytes 98308
  47.8 3.6 %copy-start.1 = (bf16[8,208,128]{2,1,0:T(8,128)(2,1)}, bf16[8,208,128]{2,1,0:T(8,128)(2,1)S(1)}, u32[]{:S(2)}) copy-start(bf16[8,208,128]{2,1,0:T(8,128)(2,1)S(1)} %all-to-all-done.2.refs_5_) | copy-start | bytes 1277956
  47.8 17.8 %all-to-all-start.1 = ((bf16[8,416,128]{2,1,0:T(8,128)(2,1)}), bf16[8,416,128]{2,1,0:T(8,128)(2,1)S(1)}, u32[]{:S(2)}, u32[]{:S(2)}) async-start(bf16[8,416,128]{2,1,0:T(8,128)(2,1)} %pick.2), calls=%async_computation.1 | async-start | bytes 1703936 | tf_op jit(solution)/shard_map/all_to_all | solution.py:335
  51.4 14.2 %collective-permute-start.1 = (bf16[8,208,128]{2,1,0:T(8,128)(2,1)S(1)}, bf16[8,208,128]{2,1,0:T(8,128)(2,1)S(1)}, u32[]{:S(2)}, u32[]{:S(2)}) collective-permute-start(bf16[8,208,128]{2,1,0:T(8,128)(2,1)S(1)} %all-to-all-done.2.refs_5_), channel_id=1, source_target_pairs={{0,1},{1,0},{2,3},{3,2},{4,5},{5,4},{6,7},{7,6},{8,9},{9,8},{10,11... | collective-permute-start | bytes 1277960 | tf_op jit(solution)/shard_map/ppermute | solution.py:353
  53.2 1.8 %copy-start.5 = (bf16[100,256]{1,0:T(8,128)(2,1)S(1)}, bf16[100,256]{1,0:T(8,128)(2,1)}, u32[]{:S(2)}) copy-start(bf16[100,256]{1,0:T(8,128)(2,1)} %param.9) | copy-start | bytes 153604
  54.1 0.7 copy-start.9
  55.1 9.9 %copy-start.10 = (s32[512]{0:T(512)S(1)}, s32[512]{0:T(512)}, u32[]{:S(2)}) copy-start(s32[512]{0:T(512)} %param.14) | copy-start | bytes 6148
  65.6 0.8 copy-start.2
  65.6 1.0 %copy-start = (bf16[8,416,128]{2,1,0:T(8,128)(2,1)}, bf16[8,416,128]{2,1,0:T(8,128)(2,1)S(1)}, u32[]{:S(2)}) copy-start(bf16[8,416,128]{2,1,0:T(8,128)(2,1)S(1)} %all-to-all-done.1.refs_4_) | copy-start | bytes 2555908

commit v5 on v4

--- a/solution.py
+++ b/solution.py
@@ -11,6 +11,7 @@
 
 LANES = 128
 DEPTH = 4
+GROUP = 16
 
 
 def spare_split(capacity, feat):
@@ -19,6 +20,10 @@
     if tucked % 8 or (capacity - tucked) % 16 or feat + piece > LANES:
         return capacity, 0, piece
     return capacity - tucked, tucked, piece
+
+
+def here(values):
+    return pltpu.with_memory_space_constraint(values, pltpu.VMEM)
 
 
 def copy_rows(index, table, out, count, start=0):
@@ -104,7 +109,7 @@
         + [pltpu.SemaphoreType.DMA((depth,))],
         out_shape=jax.ShapeDtypeStruct((peers, whole, LANES), features.dtype),
         name="pick",
-    )(wanted, features)
+    )(wanted, here(features))
 
 
 def unpack(packed, table, start, whole, capacity, piece, feat):
@@ -130,41 +135,56 @@
             table[pl.ds(base + whole, tucked), :] = extra
 
 
-def project(rows, weight, scores, heads):
-    zvals = jnp.dot(
+def project(rows, weight, scores, zvals, sums, heads):
+    zvals[...] = jnp.dot(
         rows[...].astype(jnp.bfloat16), weight[...], preferred_element_type=jnp.float32
     ).astype(jnp.bfloat16)
     parts = lax.dot_general(
-        zvals, scores[...], (((1,), (1,)), ((), ())), preferred_element_type=jnp.float32
+        zvals[...], scores[...], (((1,), (1,)), ((), ())), preferred_element_type=jnp.float32
     )
-    sums = (
+    sums[...] = (
         parts
         + pltpu.roll(parts, LANES - heads, axis=1)
         + pltpu.roll(parts, LANES - 2 * heads, axis=1)
     )
-    return zvals, sums
-
-
-def combine(zvals, sums, live, spread, heads, block, slot_total):
-    dst = pltpu.roll(sums[:block, :], LANES - 3 * heads, axis=1)
-    logits = []
-    for slot in range(slot_total):
-        logit = sums[slot * block : (slot + 1) * block, :] + dst
-        logit = jnp.maximum(logit, 0.2 * logit)
-        logits.append(jnp.where(live > slot, logit, -1e30))
-    peak = functools.reduce(jnp.maximum, logits)
-    shares = [jnp.exp(logit - peak) for logit in logits]
-    scale = 1.0 / functools.reduce(jnp.add, shares)
-    summed = None
-    for slot in range(slot_total):
-        alpha = (shares[slot] * scale).astype(jnp.bfloat16)
-        wide = jnp.dot(alpha, spread[...], preferred_element_type=jnp.float32)
-        term = wide * zvals[slot * block : (slot + 1) * block, :].astype(jnp.float32)
-        summed = term if summed is None else summed + term
-    low = jnp.minimum(summed, 0.0)
-    series = low * (1.0 + low * (0.5 + low * (1.0 / 6.0)))
-    below = jnp.where(low > -0.01, series, jnp.exp(low) - 1.0)
-    return jnp.where(summed > 0, summed, below)
+
+
+def combine(zvals, sums, live, hidden, tie, first, heads, block, slot_total):
+    group = min(GROUP, block)
+    width = zvals.shape[1]
+    lane = lax.broadcasted_iota(jnp.int32, (group, LANES), 1)
+    picks = [(lane + column * LANES) // (width // heads) for column in range(width // LANES)]
+    for start in range(0, block, group):
+        dst = pltpu.roll(sums[start : start + group, :], LANES - 3 * heads, axis=1)
+        dst = dst + 0.0 * tie[start : start + group, :]
+        alive = live[pl.ds(pl.multiple_of(first + start, 8), group), :]
+        logits = []
+        for slot in range(slot_total):
+            logit = sums[slot * block + start : slot * block + start + group, :] + dst
+            logit = jnp.maximum(logit, 0.2 * logit)
+            logits.append(jnp.where(alive > slot, logit, -1e30))
+        peak = functools.reduce(jnp.maximum, logits)
+        shares = [jnp.exp(logit - peak) for logit in logits]
+        scale = 1.0 / functools.reduce(jnp.add, shares)
+        summed = [None] * len(picks)
+        for slot in range(slot_total):
+            alpha = (shares[slot] * scale).astype(jnp.bfloat16).astype(jnp.float32)
+            for column, pick in enumerate(picks):
+                wide = jnp.take_along_axis(alpha, pick, axis=1)
+                values = zvals[
+                    slot * block + start : slot * block + start + group,
+                    column * LANES : (column + 1) * LANES,
+                ].astype(jnp.float32)
+                term = wide * values
+                summed[column] = term if summed[column] is None else summed[column] + term
+        for column, total in enumerate(summed):
+            low = jnp.minimum(total, 0.0)
+            series = low * (1.0 + low * (0.5 + low * (1.0 / 6.0)))
+            below = jnp.where(low > -0.01, series, jnp.exp(low) - 1.0)
+            hidden[
+                pl.ds(pl.multiple_of(first + start, 8), group),
+                column * LANES : (column + 1) * LANES,
+            ] = jnp.where(total > 0, total, below)
 
 
 def attend_kernel(
@@ -174,7 +194,7 @@
     nears = refs[5 : 5 + near_total]
     (
         out, table, rows_even, rows_odd, z_even, z_odd, sums_even, sums_odd, hidden,
-        raw, weight, scores, spread, live, even, odd, sems,
+        raw, weight, scores, live, even, odd, sems,
     ) = refs[5 + near_total :]
     dst_rows, width = hidden.shape
     blocks = dst_rows // block
@@ -199,7 +219,6 @@
     row = lax.broadcasted_iota(jnp.int32, (LANES, width), 0)
     owner = lax.broadcasted_iota(jnp.int32, (LANES, width), 1) // (width // heads)
     weight[...] = jnp.where(row < feat, raw[...], 0.0).astype(jnp.bfloat16)
-    spread[...] = jnp.where(row == owner, 1.0, 0.0).astype(jnp.bfloat16)
     lines = [
         jnp.where(
             row[:heads] == owner[:heads],
@@ -219,30 +238,25 @@
     unpack(far, table, base, whole, capacity, piece, feat)
 
     def first_stage(turn):
-        zvals, scored = project(rows[turn], weight, scores, heads)
-        z[turn][...] = zvals
-        sums[turn][...] = scored
+        project(rows[turn], weight, scores, z[turn], sums[turn], heads)
 
     fetch(0, 0).wait()
     copy_rows(even, table, rows_even, count)
+    first_stage(0)
     fetch(2, 0).start()
-    fetch(1, 1).wait()
-    copy_rows(odd, table, rows_odd, count)
-    fetch(3, 1).start()
-    first_stage(0)
 
     @pl.loop(0, blocks // 2)
     def _(pair):
         for turn in range(2):
             number = 2 * pair + turn
             first = pl.multiple_of(number * block, 8)
-            fetch(number + 2, turn).wait()
-            copy_rows(lists[turn], table, rows[turn], count)
+            fetch(number + 1, 1 - turn).wait()
+            copy_rows(lists[1 - turn], table, rows[1 - turn], count)
             first_stage(1 - turn)
-            hidden[pl.ds(first, block), :] = combine(
-                z[turn], sums[turn], live[pl.ds(first, block), :], spread, heads, block, slot_total
+            combine(
+                z[turn], sums[turn], live, hidden, rows[1 - turn], first, heads, block, slot_total
             )
-            fetch(number + 4, turn).start()
+            fetch(number + 3, 1 - turn).start()
 
     fetch(0, 0).wait()
     fetch(0, 1).wait()
@@ -287,7 +301,6 @@
             pltpu.VMEM((LANES, width), jnp.float32),
             pltpu.VMEM((LANES, width), jnp.bfloat16),
             pltpu.VMEM((LANES, width), jnp.bfloat16),
-            pltpu.VMEM((LANES, width), jnp.bfloat16),
             pltpu.VMEM((dst_rows, LANES), jnp.float32),
             pltpu.SMEM((count,), jnp.int32),
             pltpu.SMEM((count,), jnp.int32),
@@ -295,7 +308,7 @@
         ],
         out_shape=jax.ShapeDtypeStruct((dst_rows, out_weight.shape[1]), jnp.bfloat16),
         name="attend",
-    )(slots, shared, counts, out_weight, far, *nears)
+    )(slots, *[here(values) for values in (shared, counts, out_weight, far, *nears)])
 
 
 def three_pieces(values):
@@ -310,7 +323,27 @@
         piece.reshape(1, -1) for score in (score_src, score_dst) for piece in three_pieces(score)
     ]
     mine = jnp.concatenate([proj_weight] + pieces, axis=0)
-    return lax.all_gather(mine, "head", axis=0, tiled=False)
+    return in_order([mine] + passed_round(mine))
+
+
+def passed_round(values):
+    sides = lax.axis_size("head")
+    return [
+        lax.ppermute(values, "head", [(i, (i + step) % sides) for i in range(sides)])
+        for step in range(1, sides)
+    ]
+
+
+def in_order(turned):
+    sides = len(turned)
+    side = lax.axis_index("head")
+    if sides == 2:
+        first = side == 0
+        return jnp.stack(
+            [jnp.where(first, turned[0], turned[1]), jnp.where(first, turned[1], turned[0])]
+        )
+    stacked = jnp.stack(turned)
+    return jnp.take(stacked, (side - jnp.arange(sides)) % sides, axis=0)
 
 
 def local(
@@ -348,9 +381,7 @@
     picked = pick_rows(wanted[:, :part].reshape(-1), own, half)
     nears = [within(picked)]
     far = within(pick_rows(wanted[:, part:].reshape(-1), across, half))
-    for step in range(1, sides):
-        ring = [(i, (i + step) % sides) for i in range(sides)]
-        nears.append(lax.ppermute(nears[0], "head", ring))
+    nears += passed_round(nears[0])
 
     shared = shared_weights(proj_weight, score_src, score_dst)
     heads = score_src.shape[0] * sides

time: 81.5 us -> 75.7 us (0.929)
  waiting for transfers between devices: 18.9 us -> 29.4 us
  blocking collectives: 19.7 us -> 9.81 us
  Pallas kernels: 24.1 us -> 20.4 us
  local copies, waits for them, and re-layouts: 5.75 us -> 3.37 us
    ppermute x1 -> x2, waiting for transfers between devices: 0.01 us -> 10.4 us  [passed_round(): lax.ppermute(values, 'head', [(i, (i + step) % sides) for i in range(side...]
    all_gather x1 -> x0, blocking collectives: 9.89 us -> none  [shared_weights(): return lax.all_gather(mine, 'head', axis=0, tiled=False)]
    unnamed x27 -> x21, local copies, waits for them, and re-layouts: 4.4 us -> 2.02 us
    pallas_call x1, Pallas kernels: 14.2 us -> 12.2 us  [attend(): pl.pallas_call(functools.partial(attend_kernel, near_total=len(nears), wh...]
    pallas_call x2, Pallas kernels: 9.94 us -> 8.24 us  [pick_rows(): pl.pallas_call(functools.partial(pick_kernel, whole=whole, tucked=tucked,...]
    ppermute x1 -> x2, starting transfers between devices: 1.59 us -> 2.14 us  [passed_round(): lax.ppermute(values, 'head', [(i, (i + step) % sides) for i in range(side...]
  transfers between devices with their start and end apart: 4 -> 5, of which waited for: 1 -> 3; matrix products, arithmetic and copies ran while one was open for 3% -> 3% of each run, Pallas kernels for 7% -> 7%
where the time goes in v5:
time: 75.7 us; the launch traced here: 75.3 us
  waiting for transfers between devices  29.4 us (39%)
  Pallas kernels  20.4 us (27%)
  starting transfers between devices  12 us (16%)
  blocking collectives  9.81 us (13%)
  local copies, waits for them, and re-layouts  3.37 us (4%)
    ppermute x1, waiting for transfers between devices, local(): lax.ppermute(own, 'node', [(i, (i + half) % groups) for i in range(groups)])  18.9 us
    pallas_call x1, Pallas kernels, attend(): pl.pallas_call(functools.partial(attend_kernel, near_total=len(nears), wh...  12.2 us
    ppermute x2, waiting for transfers between devices, passed_round(): lax.ppermute(values, 'head', [(i, (i + step) % sides) for i in range(side...  10.4 us
    all_to_all x1, blocking collectives, within(): lax.all_to_all(values, 'node', split_axis=0, concat_axis=0, axis_index_gr...  9.81 us
    pallas_call x2, Pallas kernels, pick_rows(): pl.pallas_call(functools.partial(pick_kernel, whole=whole, tucked=tucked,...  8.24 us
    all_to_all x2, starting transfers between devices, within(): lax.all_to_all(values, 'node', split_axis=0, concat_axis=0, axis_index_gr...  7.17 us
    ppermute x1, starting transfers between devices, local(): lax.ppermute(own, 'node', [(i, (i + half) % groups) for i in range(groups)])  2.65 us
    ppermute x2, starting transfers between devices, passed_round(): lax.ppermute(values, 'head', [(i, (i + step) % sides) for i in range(side...  2.14 us
  transfers between devices with their start and end apart: 5, of which 3 were waited for; matrix products, arithmetic and copies ran while one was open for 3% of the time, Pallas kernels for 7%

profile of v5, /device:TPU:0, one launch (start us, length us, event | category | flops | bytes accessed | tf_op | source)
XLA Modules:
  0.0 75.3 jit_solution(13943408209073147606)
XLA Ops:
  0.0 0.8 %copy-done.3 = s32[1,16,512]{2,1,0:T(8,128)S(1)} copy-done((s32[1,16,512]{2,1,0:T(8,128)S(1)}, s32[1,16,512]{2,1,0:T(8,128)}, u32[]{:S(2)}) %copy-start.3) | copy-done | bytes 32792
  0.8 9.8 %all_to_all.15 = s32[8,6,128]{2,1,0:T(8,128)S(1)} all-to-all(s32[8,6,128]{2,1,0:T(8,128)S(1)} %copy.12), channel_id=1, replica_groups={{0,2,4,6,8,10,12,14},{16,18,20,22,24,26,28,30},{1,3,5,7,9,11,13,15},{17..., dimensions={0} | all-to-all | bytes 49152 | tf_op jit(solution)/shard_map/all_to_all | solution.py:368
  10.6 0.6 copy.15
  11.2 3.3 %pick.3 = bf16[8,208,128]{2,1,0:T(8,128)(2,1)} custom-call(s32[2048]{0:T(1024)} %bitcast.36, bf16[100,2048]{1,0:T(8,128)(2,1)S(1)} %bitcast.28), custom_call_target="tpu_custom_call" | custom-call | tf_op jit(solution)/shard_map/pick/pallas_call | solution.py:97
  14.5 3.5 %all-to-all-start.2 = ((bf16[8,208,128]{2,1,0:T(8,128)(2,1)}), bf16[8,208,128]{2,1,0:T(8,128)(2,1)S(1)}, u32[]{:S(2)}, u32[]{:S(2)}) async-start(bf16[8,208,128]{2,1,0:T(8,128)(2,1)} %pick.3), calls=%async_computation.2 | async-start | bytes 851968 | tf_op jit(solution)/shard_map/all_to_all | solution.py:368
  18.0 2.7 %collective-permute-start.1 = (bf16[100,2048]{1,0:T(8,128)(2,1)S(1)}, bf16[100,2048]{1,0:T(8,128)(2,1)S(1)}, u32[]{:S(2)}, u32[]{:S(2)}) collective-permute-start(bf16[100,2048]{1,0:T(8,128)(2,1)S(1)} %bitcast.29), channel_id=1, source_target_pairs={{0,16},{2,18},{4,20},{6,22},{8,24},{10,26},{12,28},{14,30},{16,0},... | collective-permute-start | bytes 1228808 | tf_op jit(solution)/shard_map/ppermute | solution.py:365
  20.7 0.6 copy.14
  21.3 18.9 %collective-permute-done.1.features = bf16[100,2048]{1,0:T(8,128)(2,1)S(1)} collective-permute-done((bf16[100,2048]{1,0:T(8,128)(2,1)S(1)}, bf16[100,2048]{1,0:T(8,128)(2,1)S(1)}, u32[]{:S(2)}, u32[]{:S(2)}) %collective-permute-start.1) | collective-permute-done | bytes 409632 | tf_op jit(solution)/shard_map/ppermute | solution.py:365
  40.2 5.0 %pick.2 = bf16[8,416,128]{2,1,0:T(8,128)(2,1)} custom-call(s32[4096]{0:T(1024)} %bitcast.35, bf16[100,2048]{1,0:T(8,128)(2,1)S(1)} %collective-permute-done.1.features), custom_call_target="tpu_custom_call" | custom-call | tf_op jit(solution)/shard_map/pick/pallas_call | solution.py:97
  45.3 3.7 %all-to-all-start.1 = ((bf16[8,416,128]{2,1,0:T(8,128)(2,1)}), bf16[8,416,128]{2,1,0:T(8,128)(2,1)S(1)}, u32[]{:S(2)}, u32[]{:S(2)}) async-start(bf16[8,416,128]{2,1,0:T(8,128)(2,1)} %pick.2), calls=%async_computation.1 | async-start | bytes 1703936 | tf_op jit(solution)/shard_map/all_to_all | solution.py:368
  49.0 0.1 reshape.42
  49.1 0.1 reshape.43
  49.2 0.1 reshape.44
  49.3 0.1 reshape.45
  49.3 0.1 reshape.46
  49.4 0.1 reshape.47
  49.6 1.6 %collective-permute-start = (bf16[106,256]{1,0:T(8,128)(2,1)S(1)}, bf16[106,256]{1,0:T(8,128)(2,1)S(1)}, u32[]{:S(2)}, u32[]{:S(2)}) collective-permute-start(bf16[106,256]{1,0:T(8,128)(2,1)S(1)} %concatenate.6), channel_id=1, source_target_pairs={{0,1},{1,0},{2,3},{3,2},{4,5},{5,4},{6,7},{7,6},{8,9},{9,8},{10,11... | collective-permute-start | bytes 162824 | tf_op jit(solution)/shard_map/ppermute | solution.py:332
  51.2 0.6 collective-permute-start.2
  51.8 0.1 dynamic-slice_convert_fusion
  51.8 0.1 reshape.40
  51.9 0.7 reshape.41.refs_0_
  52.6 1.2 %collective-permute-done = bf16[106,256]{1,0:T(8,128)(2,1)S(1)} collective-permute-done((bf16[106,256]{1,0:T(8,128)(2,1)S(1)}, bf16[106,256]{1,0:T(8,128)(2,1)S(1)}, u32[]{:S(2)}, u32[]{:S(2)}) %collective-permute-start) | collective-permute-done | bytes 54304 | tf_op jit(solution)/shard_map/ppermute | solution.py:332
  53.9 9.2 %collective-permute-done.2.refs_6_ = bf16[8,208,128]{2,1,0:T(8,128)(2,1)S(1)} collective-permute-done((bf16[8,208,128]{2,1,0:T(8,128)(2,1)S(1)}, bf16[8,208,128]{2,1,0:T(8,128)(2,1)S(1)}, u32[]{:S(2)}, u32[]{:S(2)}) %collective-permute-start.2) | collective-permute-done | bytes 426016 | tf_op jit(solution)/shard_map/ppermute | solution.py:332
  63.1 12.2 %attend.1 = bf16[256,512]{1,0:T(8,128)(2,1)} custom-call(s32[4096]{0:T(1024)} %reshape.41.refs_0_, bf16[2,106,256]{2,1,0:T(8,128)(2,1)S(1)} %pad_maximum_fusion.refs_1_, f32[1,256]{1,0:T(1,128)S(1)} %bitcast.30, bf16[512,512]{1,0:T(8,128)(2,1)S(1)} %copy-done, bf16[8,416,128]{2,1,0:T(8,128)(2,1)S(1)} %all-to-all-done.1.refs_4_, ...), custom_call_target="tpu_custom_call" | custom-call | tf_op jit(solution)/shard_map/attend/pallas_call | solution.py:275
  (32 shorter events, 0.3 us)
Async XLA Ops:
  0.0 0.8 %copy-start.3 = (s32[1,16,512]{2,1,0:T(8,128)S(1)}, s32[1,16,512]{2,1,0:T(8,128)}, u32[]{:S(2)}) copy-start(s32[1,16,512]{2,1,0:T(8,128)} %param.12) | copy-start | bytes 98308
  0.0 11.2 %copy-start.1 = (bf16[2048,100]{0,1:T(8,128)(2,1)S(1)}, bf16[2048,100]{0,1:T(8,128)(2,1)}, u32[]{:S(2)}) copy-start(bf16[2048,100]{0,1:T(8,128)(2,1)} %param.8) | copy-start | bytes 1228804
  14.5 30.7 %all-to-all-start.2 = ((bf16[8,208,128]{2,1,0:T(8,128)(2,1)}), bf16[8,208,128]{2,1,0:T(8,128)(2,1)S(1)}, u32[]{:S(2)}, u32[]{:S(2)}) async-start(bf16[8,208,128]{2,1,0:T(8,128)(2,1)} %pick.3), calls=%async_computation.2 | async-start | bytes 851968 | tf_op jit(solution)/shard_map/all_to_all | solution.py:368
  18.0 22.2 %collective-permute-start.1 = (bf16[100,2048]{1,0:T(8,128)(2,1)S(1)}, bf16[100,2048]{1,0:T(8,128)(2,1)S(1)}, u32[]{:S(2)}, u32[]{:S(2)}) collective-permute-start(bf16[100,2048]{1,0:T(8,128)(2,1)S(1)} %bitcast.29), channel_id=1, source_target_pairs={{0,16},{2,18},{4,20},{6,22},{8,24},{10,26},{12,28},{14,30},{16,0},... | collective-permute-start | bytes 1228808 | tf_op jit(solution)/shard_map/ppermute | solution.py:365
  45.2 3.8 %copy-start.5 = (f32[4,64]{1,0:T(4,128)S(1)}, f32[4,64]{1,0:T(4,128)}, u32[]{:S(2)}) copy-start(f32[4,64]{1,0:T(4,128)} %param.10) | copy-start | bytes 3076
  45.2 4.0 %copy-start.6 = (f32[4,64]{1,0:T(4,128)S(1)}, f32[4,64]{1,0:T(4,128)}, u32[]{:S(2)}) copy-start(f32[4,64]{1,0:T(4,128)} %param.11) | copy-start | bytes 3076
  45.2 4.3 %copy-start.2 = (bf16[100,256]{1,0:T(8,128)(2,1)S(1)}, bf16[100,256]{1,0:T(8,128)(2,1)}, u32[]{:S(2)}) copy-start(bf16[100,256]{1,0:T(8,128)(2,1)} %param.9) | copy-start | bytes 153604
  45.2 5.9 %copy-start.4 = (s32[512,16]{0,1:T(8,128)S(1)}, s32[512,16]{0,1:T(8,128)}, u32[]{:S(2)}) copy-start(s32[512,16]{0,1:T(8,128)} %param.13) | copy-start | bytes 98308
  45.2 6.5 %copy-start.7 = (s32[512]{0:T(512)S(1)}, s32[512]{0:T(512)}, u32[]{:S(2)}) copy-start(s32[512]{0:T(512)} %param.14) | copy-start | bytes 6148
  45.3 17.8 %all-to-all-start.1 = ((bf16[8,416,128]{2,1,0:T(8,128)(2,1)}), bf16[8,416,128]{2,1,0:T(8,128)(2,1)S(1)}, u32[]{:S(2)}, u32[]{:S(2)}) async-start(bf16[8,416,128]{2,1,0:T(8,128)(2,1)} %pick.2), calls=%async_computation.1 | async-start | bytes 1703936 | tf_op jit(solution)/shard_map/all_to_all | solution.py:368
  49.0 14.1 %copy-start = (bf16[512,512]{1,0:T(8,128)(2,1)S(1)}, bf16[512,512]{1,0:T(8,128)(2,1)}, u32[]{:S(2)}) copy-start(bf16[512,512]{1,0:T(8,128)(2,1)} %refs_3_.1) | copy-start | bytes 1572868
  49.6 4.3 %collective-permute-start = (bf16[106,256]{1,0:T(8,128)(2,1)S(1)}, bf16[106,256]{1,0:T(8,128)(2,1)S(1)}, u32[]{:S(2)}, u32[]{:S(2)}) collective-permute-start(bf16[106,256]{1,0:T(8,128)(2,1)S(1)} %concatenate.6), channel_id=1, source_target_pairs={{0,1},{1,0},{2,3},{3,2},{4,5},{5,4},{6,7},{7,6},{8,9},{9,8},{10,11... | collective-permute-start | bytes 162824 | tf_op jit(solution)/shard_map/ppermute | solution.py:332
  51.2 11.9 %collective-permute-start.2 = (bf16[8,208,128]{2,1,0:T(8,128)(2,1)S(1)}, bf16[8,208,128]{2,1,0:T(8,128)(2,1)S(1)}, u32[]{:S(2)}, u32[]{:S(2)}) collective-permute-start(bf16[8,208,128]{2,1,0:T(8,128)(2,1)S(1)} %all-to-all-done.2.refs_5_), channel_id=1, source_target_pairs={{0,1},{1,0},{2,3},{3,2},{4,5},{5,4},{6,7},{7,6},{8,9},{9,8},{10,11... | collective-permute-start | bytes 1277960 | tf_op jit(solution)/shard_map/ppermute | solution.py:332
